TPU v7x, 8 devices: a whole 2x2x1 slice. The times are simulated.
8 devices in a mesh: dp: 1 (over z), hid: 2 (over y), tp: 4 (over x, core).
Axes of the slice: x: 2, y: 2, z: 1, core: 2. Of those that a mesh axis runs over, the one named last changes fastest.
Arguments:
- hidden: bfloat16 [1024, 2048], P('dp', 'hid')
- rms_attn: float32 [2048], P('hid')
- rms_mlp: float32 [2048], P('hid')
- w_q: bfloat16 [2048, 2048], P('hid', 'tp')
- w_k: bfloat16 [2048, 512], P('hid', 'tp')
- w_v: bfloat16 [2048, 512], P('hid', 'tp')
- w_o: bfloat16 [2048, 2048], P('tp', 'hid')
- w_gate: bfloat16 [2048, 8192], P('hid', 'tp')
- w_up: bfloat16 [2048, 8192], P('hid', 'tp')
- w_down: bfloat16 [8192, 2048], P('tp', 'hid')
- k_cache: bfloat16 [2048, 8, 64], P('dp', 'tp')
- v_cache: bfloat16 [2048, 8, 64], P('dp', 'tp')
- past_len: int32 [1], P('dp')
Outputs:
- output 1: bfloat16 [1024, 2048], P('dp', 'hid')
- output 2: bfloat16 [2048, 8, 64], P('dp', 'tp')
- output 3: bfloat16 [2048, 8, 64], P('dp', 'tp')
All inputs are finite; a program needn't handle non-finite values.
Results may differ from a plain program's by a relative error of at most 0.0148705.
Values are sent between devices in bfloat16 or wider.
A program may use at most 1 GiB of HBM per device.

v0:
```python
import math
import jax
import jax.numpy as jnp
from jax import lax
from jax.sharding import PartitionSpec as P

ROPE_BASE = 10000.0


def rope_tables(pos_start, length, head_dim):
    positions = (pos_start + jnp.arange(length)).astype(jnp.float32)
    inv_freq = jnp.exp(jnp.arange(head_dim // 2, dtype=jnp.float32) * (-2.0 * math.log(ROPE_BASE) / head_dim))
    angles = positions[:, None] * inv_freq[None, :]
    return jnp.cos(angles)[:, None, :], jnp.sin(angles)[:, None, :]


def apply_rope(x_in, cos_t, sin_t):
    x_f32 = x_in.astype(jnp.float32)
    half_dim = x_f32.shape[-1] // 2
    x_first = x_f32[..., :half_dim]
    x_second = x_f32[..., half_dim:]
    rotated = jnp.concatenate([x_first * cos_t - x_second * sin_t, x_second * cos_t + x_first * sin_t], axis=-1)
    return rotated.astype(jnp.bfloat16)


def attend(q_rot, k_full, v_full, pos_start):
    new_len = q_rot.shape[0]
    n_heads = q_rot.shape[1]
    head_dim = q_rot.shape[2]
    t_len = k_full.shape[0]
    kv_heads = k_full.shape[1]
    q_grp = q_rot.reshape(new_len, kv_heads, n_heads // kv_heads, head_dim)
    scores = jnp.einsum('cgrd,tgd->grct', q_grp, k_full, preferred_element_type=jnp.float32) * (head_dim ** -0.5)
    causal = jnp.arange(t_len)[None, :] <= (pos_start + jnp.arange(new_len))[:, None]
    attn_probs = jax.nn.softmax(jnp.where(causal, scores, -1e30), axis=-1).astype(jnp.bfloat16)
    head_mix = jnp.einsum('grct,tgd->cgrd', attn_probs, v_full, preferred_element_type=jnp.float32)
    return head_mix.astype(jnp.bfloat16).reshape(new_len, n_heads * head_dim)


def solution(mesh):
    hid_n = mesh.shape['hid']
    tp_n = mesh.shape['tp']

    def local_layer(hidden, rms_attn, rms_mlp, w_q, w_k, w_v, w_o, w_gate, w_up, w_down, k_cache, v_cache, past_len):
        new_len = hidden.shape[0]
        d_model = hidden.shape[1] * hid_n
        head_dim = k_cache.shape[2]
        kv_local = k_cache.shape[1]
        q_local = w_q.shape[1] // head_dim
        rows_per = new_len // tp_n
        pos_start = past_len[0]
        hid_f32 = hidden.astype(jnp.float32)
        sq_first = lax.psum(jnp.sum(hid_f32 * hid_f32, axis=1, keepdims=True), 'hid')
        u_attn = (hid_f32 * lax.rsqrt(sq_first / d_model + 1e-5) * rms_attn).astype(jnp.bfloat16)
        q_part = jnp.dot(u_attn, w_q, preferred_element_type=jnp.float32).astype(jnp.bfloat16)
        k_part = jnp.dot(u_attn, w_k, preferred_element_type=jnp.float32).astype(jnp.bfloat16)
        v_part = jnp.dot(u_attn, w_v, preferred_element_type=jnp.float32).astype(jnp.bfloat16)
        q_sum, k_sum, v_sum = lax.psum((q_part, k_part, v_part), 'hid')
        cos_t, sin_t = rope_tables(pos_start, new_len, head_dim)
        q_rot = apply_rope(q_sum.reshape(new_len, q_local, head_dim), cos_t, sin_t)
        k_rot = apply_rope(k_sum.reshape(new_len, kv_local, head_dim), cos_t, sin_t)
        k_full = lax.dynamic_update_slice(k_cache, k_rot, (pos_start, 0, 0))
        v_full = lax.dynamic_update_slice(v_cache, v_sum.reshape(new_len, kv_local, head_dim), (pos_start, 0, 0))
        head_mix = attend(q_rot, k_full, v_full, pos_start)
        attn_part = jnp.dot(head_mix, w_o, preferred_element_type=jnp.float32).astype(jnp.bfloat16)
        attn_rows = lax.psum_scatter(attn_part, 'tp', scatter_dimension=0, tiled=True)
        own_rows = lax.dynamic_slice_in_dim(hidden, lax.axis_index('tp') * rows_per, rows_per, axis=0)
        mid_rows = (own_rows.astype(jnp.float32) + attn_rows.astype(jnp.float32)).astype(jnp.bfloat16)
        mid_f32 = mid_rows.astype(jnp.float32)
        sq_second = lax.psum(jnp.sum(mid_f32 * mid_f32, axis=1, keepdims=True), 'hid')
        u_rows = (mid_f32 * lax.rsqrt(sq_second / d_model + 1e-5) * rms_mlp).astype(jnp.bfloat16)
        u_mlp = lax.all_gather(u_rows, 'tp', axis=0, tiled=True)
        gate_part = jnp.dot(u_mlp, w_gate, preferred_element_type=jnp.float32).astype(jnp.bfloat16)
        up_part = jnp.dot(u_mlp, w_up, preferred_element_type=jnp.float32).astype(jnp.bfloat16)
        gate_sum, up_sum = lax.psum((gate_part, up_part), 'hid')
        activated = (jax.nn.silu(gate_sum.astype(jnp.float32)) * up_sum.astype(jnp.float32)).astype(jnp.bfloat16)
        down_part = jnp.dot(activated, w_down, preferred_element_type=jnp.float32).astype(jnp.bfloat16)
        down_rows = lax.psum_scatter(down_part, 'tp', scatter_dimension=0, tiled=True)
        out_rows = (mid_f32 + down_rows.astype(jnp.float32)).astype(jnp.bfloat16)
        layer_out = lax.all_gather(out_rows, 'tp', axis=0, tiled=True)
        return layer_out, k_full, v_full

    row_split = P('hid', 'tp')
    col_split = P('tp', 'hid')
    cache_spec = P('dp', 'tp', None)
    in_specs = (P('dp', 'hid'), P('hid'), P('hid'), row_split, row_split, row_split, col_split,
                row_split, row_split, col_split, cache_spec, cache_spec, P('dp'))
    out_specs = (P('dp', 'hid'), cache_spec, cache_spec)
    return jax.shard_map(local_layer, mesh=mesh, in_specs=in_specs, out_specs=out_specs, check_vma=False)
```

profile of v0, /device:TPU:0, one launch (start us, length us, event | category | flops | bytes accessed | tf_op | source)
XLA Modules:
  0.0 470.3 jit_solution(4448558159659287284)
XLA Ops:
  7.2 0.0 copy-start
  7.2 0.0 copy-start.1
  7.2 0.0 copy-start.7
  7.2 0.0 all-reduce.7.cloned.1.call-start
  7.2 2.0 copy.32
  9.3 1.9 copy.33
  11.2 0.0 copy-start.5
  11.2 2.1 fusion.13
  13.3 6.3 %psum.49 = f32[1024,1]{0,1:T(1,128)S(1)} all-reduce(f32[1024,1]{0,1:T(1,128)S(1)} %bitcast.61), channel_id=1, replica_groups=mesh['dp'=1,'hid'=2,'tp'=4] {'hid'}, use_global_device_ids=true, to_apply=%region_1.0 | all-reduce | flops 1024 | bytes 8192 | tf_op jit(solution)/shard_map/psum | solution.py:53
  19.6 0.0 copy-done.1
  19.6 0.0 copy-done.7
  19.6 0.0 copy-start.6
  19.6 3.7 convolution_convert_fusion.3
  23.3 0.0 copy-done.5
  23.3 1.6 convolution_convert_fusion.5
  24.9 0.0 copy-done.6
  24.9 1.6 convolution_convert_fusion.4
  26.5 0.0 all-reduce.7.cloned.1.call-update
  26.5 0.2 reduce-scatter.3.cloned.1.call-start
  27.4 0.5 multiply_cosine_fusion
  28.0 1.8 iota_compare_fusion
  29.8 44.1 %all-reduce.7.cloned.1.call-done = (bf16[1024,8,64]{0,2,1:T(8,128)(2,1)}, bf16[1024,2,64]{0,2,1:T(8,128)(2,1)}, bf16[1024,2,64]{0,2,1:T(8,128)(2,1)}) async-done(((bf16[1024,8,64]{0,2,1:T(8,128)(2,1)}, bf16[1024,2,64]{0,2,1:T(8,128)(2,1)}, bf16[1024,2,64]{0,2,1:T(8,128)(2,1)}), (bf16[1024,8,64]{0,2,1:T(8,128)(2,1)}, bf16[1024,2,64]{0,2,1:T(8,128)(2,1)}, ...) | async-done | bytes 1572880 | tf_op jit(solution)/shard_map/psum | solution.py:58
  73.9 1.0 convert_element_type.94
  74.9 1.5 convert_element_type.98
  76.4 0.1 subtract_convert_fusion.1
  76.5 1.3 subtract_convert_fusion
  77.8 3.4 dynamic_update_slice.7
  81.2 3.5 dynamic_update_slice.6
  84.6 31.4 %fusion.43 = (f32[2,4,1024]{2,1,0:T(4,128)S(1)}, f32[2,4,1024,2048]{2,3,1,0:T(8,128)}) fusion(pred[1024,2048]{0,1:T(8,128)(4,1)S(1)} %iota_compare_fusion, bf16[1024,2,4,32]{0,3,2,1:T(8,128)(2,1)} %bitcast.58, bf16[1024,2,4,32]{0,3,2,1:T(8,128)(2,1)} %bitcast.57, bf16[2048,2,64]{0,2,1:T(8,128)(2,1)} %dynamic_update_slice.7), kind=kOutput, calls=%fused_computation.62 | convolution fusion | flops 2216691712 | bytes 70811648 | tf_op jit(solution)/shard_map/sub | solution.py:35
  116.0 22.1 %fusion.21 = bf16[2,64,4,1024]{3,1,2,0:T(8,128)(2,1)S(1)} fusion(f32[2,4,1024,2048]{2,3,1,0:T(8,128)} %get-tuple-element.17, f32[2,4,1024]{2,1,0:T(4,128)S(1)} %get-tuple-element.16, bf16[2048,2,64]{0,2,1:T(8,128)(2,1)} %dynamic_update_slice.6), kind=kOutput, calls=%fused_computation.32 | convolution fusion | flops 2181562368 | bytes 68714496 | tf_op jit(solution)/shard_map/grct,tgd->cgrd/dot_general | solution.py:36
  138.2 0.0 copy-done
  138.2 0.0 copy-start.2
  138.2 2.6 convolution_convert_fusion.2
  140.8 0.0 reduce-scatter.3.cloned.1.call-update
  140.8 0.3 all-gather.3.cloned.1.call-start
  141.1 25.4 %reduce-scatter.3.cloned.1.call-done = bf16[256,1024]{1,0:T(8,128)(2,1)} async-done(((bf16[1024,1024]{1,0:T(8,128)(2,1)}), bf16[256,1024]{1,0:T(8,128)(2,1)}) %reduce-scatter.3.cloned.1.call-update) | async-done | bytes 524304 | tf_op jit(solution)/shard_map/reduce_scatter | solution.py:66
  166.5 1.5 fusion.22
  168.0 4.9 %psum.53 = f32[256,1]{0,1:T(1,128)S(1)} all-reduce(f32[256,1]{0,1:T(1,128)S(1)} %bitcast.62), channel_id=1, replica_groups=mesh['dp'=1,'hid'=2,'tp'=4] {'hid'}, use_global_device_ids=true, to_apply=%region_9.10 | all-reduce | flops 256 | bytes 2048 | tf_op jit(solution)/shard_map/psum | solution.py:70
  172.9 0.0 copy-done.2
  172.9 1.0 fusion.24
  173.9 0.0 all-gather.3.cloned.1.call-update
  173.9 0.0 all-reduce.5.cloned.1.call-start
  174.0 19.7 %all-gather.3.cloned.1.call-done = bf16[1024,1024]{1,0:T(8,128)(2,1)} async-done(((bf16[256,1024]{1,0:T(8,128)(2,1)}), bf16[1024,1024]{1,0:T(8,128)(2,1)}) %all-gather.3.cloned.1.call-update) | async-done | bytes 2097168 | tf_op jit(solution)/shard_map/all_gather | solution.py:72
  193.7 0.0 copy-start.3
  193.7 0.0 copy-start.4
  193.7 9.4 %convolution_convert_fusion = bf16[1024,2048]{1,0:T(8,128)(2,1)} fusion(bf16[1024,1024]{1,0:T(8,128)(2,1)} %all-gather.3.cloned.1.call-done, bf16[1024,2048]{1,0:T(8,128)(2,1)} %param.21), kind=kOutput, calls=%fused_computation.24 | convolution fusion | flops 4297064448 | bytes 10485760 | tf_op jit(solution)/shard_map/dot_general | solution.py:74
  203.1 0.0 copy-done.3
  203.1 0.0 copy-done.4
  203.1 6.1 %convolution_convert_fusion.1 = bf16[1024,2048]{1,0:T(8,128)(2,1)} fusion(bf16[1024,1024]{1,0:T(8,128)(2,1)S(1)} %copy-done.4, bf16[1024,2048]{1,0:T(8,128)(2,1)S(1)} %copy-done.3), kind=kOutput, calls=%fused_computation.25 | convolution fusion | flops 4297064448 | bytes 10485760 | tf_op jit(solution)/shard_map/dot_general | solution.py:73
  209.2 0.0 all-reduce.5.cloned.1.call-update
  209.2 0.0 reduce-scatter.5.cloned.1.call-start
  209.2 192.3 %all-reduce.5.cloned.1.call-done = (bf16[1024,2048]{1,0:T(8,128)(2,1)}, bf16[1024,2048]{1,0:T(8,128)(2,1)}) async-done(((bf16[1024,2048]{1,0:T(8,128)(2,1)}, bf16[1024,2048]{1,0:T(8,128)(2,1)}), (bf16[1024,2048]{1,0:T(8,128)(2,1)}, bf16[1024,2048]{1,0:T(8,128)(2,1)})) %all-reduce.5.cloned.1.call-update) | async-done | bytes 8388624 | tf_op jit(solution)/shard_map/psum | solution.py:75
  401.5 11.0 %fusion.18 = bf16[1024,1024]{1,0:T(8,128)(2,1)} fusion(bf16[2048,1024]{1,0:T(8,128)(2,1)} %param.22, bf16[1024,2048]{1,0:T(8,128)(2,1)} %get-tuple-element.3, bf16[1024,2048]{1,0:T(8,128)(2,1)} %get-tuple-element.4), kind=kOutput, calls=%fused_computation.27 | convolution fusion | flops 4312793088 | bytes 14680064 | tf_op jit(solution)/shard_map/dot_general | solution.py:77
  412.6 0.0 reduce-scatter.5.cloned.1.call-update
  412.6 0.0 all-gather.5.cloned.1.call-start
  412.6 26.0 %reduce-scatter.5.cloned.1.call-done = bf16[256,1024]{1,0:T(8,128)(2,1)} async-done(((bf16[1024,1024]{1,0:T(8,128)(2,1)}), bf16[256,1024]{1,0:T(8,128)(2,1)}) %reduce-scatter.5.cloned.1.call-update) | async-done | bytes 524304 | tf_op jit(solution)/shard_map/reduce_scatter | solution.py:78
  438.6 2.0 fusion.25
  440.6 0.0 all-gather.5.cloned.1.call-update
  440.6 19.7 %all-gather.5.cloned.1.call-done = bf16[1024,1024]{1,0:T(8,128)(2,1)} async-done(((bf16[256,1024]{1,0:T(8,128)(2,1)}), bf16[1024,1024]{1,0:T(8,128)(2,1)}) %all-gather.5.cloned.1.call-update) | async-done | bytes 2097168 | tf_op jit(solution)/shard_map/all_gather | solution.py:80
  460.4 3.1 copy.34
  (5 shorter events, 0.1 us)
Async XLA Ops:
  7.2 131.0 %copy-start = (bf16[512,1024]{1,0:T(8,128)(2,1)S(1)}, bf16[512,1024]{1,0:T(8,128)(2,1)}, u32[]{:S(2)}) copy-start(bf16[512,1024]{1,0:T(8,128)(2,1)} %param.19) | copy-start | bytes 3145732
  7.2 12.4 %copy-start.1 = (bf16[1024,1024]{1,0:T(8,128)(2,1)S(1)}, bf16[1024,1024]{1,0:T(8,128)(2,1)}, u32[]{:S(2)}) copy-start(bf16[1024,1024]{1,0:T(8,128)(2,1)} %param.13) | copy-start | bytes 6291460
  7.2 12.4 %copy-start.7 = (f32[1024]{0:T(1024)S(1)}, f32[1024]{0:T(1024)}, u32[]{:S(2)}) copy-start(f32[1024]{0:T(1024)} %param.14) | copy-start | bytes 12292
  7.2 66.7 %all-reduce.7.cloned.1.call-start = ((), (), s32[]{:S(2)}) async-start(), calls=%async_computation.7 | async-start | bytes 3145728 | tf_op jit(solution)/shard_map/psum | solution.py:58
  11.2 12.1 %copy-start.5 = (bf16[1024,128]{1,0:T(8,128)(2,1)S(1)}, bf16[1024,128]{1,0:T(8,128)(2,1)}, u32[]{:S(2)}) copy-start(bf16[1024,128]{1,0:T(8,128)(2,1)} %param.18) | copy-start | bytes 786436
  19.6 5.3 %copy-start.6 = (bf16[1024,128]{1,0:T(8,128)(2,1)S(1)}, bf16[1024,128]{1,0:T(8,128)(2,1)}, u32[]{:S(2)}) copy-start(bf16[1024,128]{1,0:T(8,128)(2,1)} %param.17) | copy-start | bytes 786436
  26.5 140.0 %reduce-scatter.3.cloned.1.call-start = ((), (), s32[]{:S(2)}) async-start(), calls=%async_computation.2 | async-start | bytes 2621440 | tf_op jit(solution)/shard_map/reduce_scatter | solution.py:66
  138.2 34.7 %copy-start.2 = (f32[1024]{0:T(1024)S(1)}, f32[1024]{0:T(1024)}, u32[]{:S(2)}) copy-start(f32[1024]{0:T(1024)} %param.15) | copy-start | bytes 12292
  140.8 52.8 %all-gather.3.cloned.1.call-start = ((), (), s32[]{:S(2)}) async-start(), calls=%async_computation.3 | async-start | bytes 2621440 | tf_op jit(solution)/shard_map/all_gather | solution.py:72
  173.9 227.6 %all-reduce.5.cloned.1.call-start = ((), (), s32[]{:S(2)}) async-start(), calls=%async_computation.6 | async-start | bytes 16777216 | tf_op jit(solution)/shard_map/psum | solution.py:75
  193.7 9.4 %copy-start.3 = (bf16[1024,2048]{1,0:T(8,128)(2,1)S(1)}, bf16[1024,2048]{1,0:T(8,128)(2,1)}, u32[]{:S(2)}) copy-start(bf16[1024,2048]{1,0:T(8,128)(2,1)} %param.20) | copy-start | bytes 12582916
  193.7 9.4 %copy-start.4 = (bf16[1024,1024]{1,0:T(8,128)(2,1)S(1)}, bf16[1024,1024]{1,0:T(8,128)(2,1)}, u32[]{:S(2)}) copy-start(bf16[1024,1024]{1,0:T(8,128)(2,1)} %all-gather.3.cloned.1.call-done) | copy-start | bytes 6291460
  209.2 229.4 %reduce-scatter.5.cloned.1.call-start = ((), (), s32[]{:S(2)}) async-start(), calls=%async_computation.4 | async-start | bytes 2621440 | tf_op jit(solution)/shard_map/reduce_scatter | solution.py:78
  412.6 47.8 %all-gather.5.cloned.1.call-start = ((), (), s32[]{:S(2)}) async-start(), calls=%async_computation.5 | async-start | bytes 2621440 | tf_op jit(solution)/shard_map/all_gather | solution.py:80
Sparse Core Ops, SparseCore 0:
  26.6 47.2 all-reduce.6
  141.0 25.5 reduce-scatter.2
  174.1 19.5 all-gather.2
  209.3 192.1 all-reduce.4
  412.7 25.8 reduce-scatter.4
  440.8 19.5 all-gather.4
where the time goes:
time: 471 us; the launch traced here: 470 us
  waiting for transfers between devices  327 us (69%)
  matrix products  89.5 us (19%)
  between operations  14.9 us (3%)
  local copies, waits for them, and re-layouts  13.9 us (3%)
  other arithmetic  12.8 us (3%)
  blocking collectives  11.2 us (2%)
    psum x1, waiting for transfers between devices, local_layer(): gate_sum, up_sum = lax.psum((gate_part, up_part), 'hid')  192 us
    psum x1, waiting for transfers between devices, local_layer(): q_sum, k_sum, v_sum = lax.psum((q_part, k_part, v_part), 'hid')  44.1 us
    sub x1, matrix products, attend(): jax.nn.softmax(jnp.where(causal, scores, -1e+30), axis=-1)  31.4 us
    reduce_scatter x1, waiting for transfers between devices, local_layer(): lax.psum_scatter(down_part, 'tp', scatter_dimension=0, tiled=True)  26 us
    reduce_scatter x1, waiting for transfers between devices, local_layer(): lax.psum_scatter(attn_part, 'tp', scatter_dimension=0, tiled=True)  25.4 us
    dot_general x1, matrix products, attend(): jnp.einsum('grct,tgd->cgrd', attn_probs, v_full, preferred_element_type=j...  22.1 us
    all_gather x1, waiting for transfers between devices, local_layer(): layer_out = lax.all_gather(out_rows, 'tp', axis=0, tiled=True)  19.7 us
    all_gather x1, waiting for transfers between devices, local_layer(): u_mlp = lax.all_gather(u_rows, 'tp', axis=0, tiled=True)  19.7 us
  transfers between devices with their start and end apart: 6, of which 6 were waited for; matrix products, arithmetic and copies ran while one was open for 0% of the time, Pallas kernels for 0%

commit v1 on v0

v1 whole, which is shorter than its diff:
```python
import math
import jax
import jax.numpy as jnp
from jax import lax
from jax.experimental import pallas as pl
from jax.experimental.pallas import tpu as pltpu
from jax.sharding import PartitionSpec as P

ROPE_BASE = 10000.0
F32, BF16 = jnp.float32, jnp.bfloat16
NEG = -1e30
BLK = 256
HALF = BLK // 2
PAST_MAX = 1024
NB = 4
CH = 4
CW = 256
MESH = pl.DeviceIdType.MESH
NT = (((1,), (1,)), ((), ()))

Q, R, O, C, X, D, T, E, Y, F, G, A = 0, 4, 5, 9, 13, 17, 21, 25, 29, 33, 37, 53
N_REMOTE = 69


def rope(t, cos_t, sin_t):
    width = t.shape[1]
    lane = lax.broadcasted_iota(jnp.int32, t.shape, 1)
    swapped = jnp.where((lane & 63) < 32, pltpu.roll(t, width - 32, 1), pltpu.roll(t, 32, 1))
    cos_w = jnp.concatenate([cos_t] * (width // 128), axis=1)
    sin_w = jnp.concatenate([sin_t] * (width // 128), axis=1)
    return (t * cos_w + swapped * sin_w).astype(BF16)


def row_sums(t):
    sq = jnp.broadcast_to(jnp.sum(t * t, axis=1, keepdims=True), (t.shape[0], 128))
    return jnp.transpose(sq)[:8]


def as_column(row):
    return jnp.transpose(jnp.broadcast_to(row[:1], (128, row.shape[1])))[:, :1]


def kernel(d_model, p_ref, x_hbm, g1_ref, g2_ref, freq_ref, wq_hbm, wk_hbm, wv_hbm, wo_hbm, wg_hbm, wu_hbm, wd_hbm, kc_hbm, vc_hbm,
           out_hbm, ko_hbm, vo_hbm,
           x, wq, wk, wv, wo, wg, wu, wd, kc, vc, qsend, qkeep, qrecv, sq1, sq1r, cos_b, sin_b, kk, vv, qs, kvn, ob, orecv,
           csend, ckeep, crecv, part, xrecv, mid, sq2, sq2r, hg, gsend, gkeep, grecv, ab, arecv, acc,
           esend, ekeep, erecv, part2, yrecv, fin, lsem, osem, ssem, rsem):
    h = lax.axis_index('hid')
    t = lax.axis_index('tp')
    c = lax.rem(t, 2)
    hid_dev = {'hid': 1 - h}
    core_dev = {'tp': t + 1 - 2 * c}
    x_dev = {'tp': lax.rem(t + 2, 4)}
    own = h == 0

    loads = []

    def load(src, dst):
        n = len(loads)
        cp = pltpu.make_async_copy(src, dst, lsem.at[n])
        cp.start()
        loads.append(cp)
        return cp

    ld_x = [load(x_hbm.at[pl.ds(0, BLK)], x.at[pl.ds(0, BLK)])]
    ld_q = [load(wq_hbm, wq), load(wk_hbm, wk), load(wv_hbm, wv)]
    ld_x += [load(x_hbm.at[pl.ds(i * BLK, BLK)], x.at[pl.ds(i * BLK, BLK)]) for i in range(1, NB)]
    ld_kc, ld_vc = load(kc_hbm, kc), load(vc_hbm, vc)
    ld_wo = load(wo_hbm, wo)
    ld_gu = [load(wg_hbm, wg), load(wu_hbm, wu)]
    ld_wd = load(wd_hbm, wd)

    barrier = pltpu.get_barrier_semaphore()
    for dev in (hid_dev, core_dev, x_dev):
        pl.semaphore_signal(barrier, inc=1, device_id=dev, device_id_type=MESH)
    pl.semaphore_wait(barrier, 3)

    def remote(src, dst, n, dev):
        return pltpu.make_async_remote_copy(src_ref=src, dst_ref=dst, send_sem=ssem.at[n], recv_sem=rsem.at[n],
                                            device_id=dev, device_id_type=MESH)

    def q_copy(i): return remote(qsend.at[i], qrecv.at[i], Q + i, hid_dev)
    def r_copy(): return remote(sq1, sq1r, R, hid_dev)
    def o_copy(i): return remote(ob.at[i], orecv.at[i], O + i, hid_dev)
    def c_copy(i): return remote(csend.at[i], crecv.at[i], C + i, core_dev)
    def x_copy(i): return remote(part.at[i], xrecv.at[i], X + i, x_dev)
    def d_copy(i): return remote(mid.at[i, 0], mid.at[i, 1], D + i, core_dev)
    def t_copy(i): return remote(sq2.at[i], sq2r.at[i], T + i, hid_dev)
    def g_copy(i, j): return remote(gsend.at[i, j], grecv.at[i, j], G + CH * i + j, hid_dev)
    def a_copy(i, j): return remote(ab.at[i, j], arecv.at[i, j], A + CH * i + j, hid_dev)
    def e_copy(i): return remote(esend.at[i], erecv.at[i], E + i, core_dev)
    def y_copy(i): return remote(part2.at[i], yrecv.at[i], Y + i, x_dev)
    def f_copy(i): return remote(fin.at[i, 0], fin.at[i, 1], F + i, core_dev)

    def qkv(i):
        xf = x[pl.ds(i * BLK, BLK), :].astype(F32)
        sq1[:, i * BLK:(i + 1) * BLK] = row_sums(xf)
        xg = (xf * g1_ref[...]).astype(BF16)
        q = jnp.dot(xg, wq[...], preferred_element_type=F32).astype(BF16)
        qsend[i, :, :256] = jnp.where(own, q[:, 256:], q[:, :256])
        qkeep[i] = jnp.where(own, q[:, :256], q[:, 256:])
        qsend[i, :, 256:384] = jnp.dot(xg, wk[...], preferred_element_type=F32).astype(BF16)
        qsend[i, :, 384:] = jnp.dot(xg, wv[...], preferred_element_type=F32).astype(BF16)

    def tables(i):
        pos = (p_ref[0] + i * BLK + lax.broadcasted_iota(jnp.int32, (BLK, 128), 0)).astype(F32)
        ang = pos * freq_ref[...]
        lane = lax.broadcasted_iota(jnp.int32, (BLK, 128), 1)
        cos_b[pl.ds(i * BLK, BLK), :] = jnp.cos(ang)
        sin = jnp.sin(ang)
        sin_b[pl.ds(i * BLK, BLK), :] = jnp.where((lane & 63) < 32, -sin, sin)

    def att(i):
        rows = slice(i * BLK, (i + 1) * BLK)
        q_copy(i).wait_recv()
        r = as_column(lax.rsqrt((sq1[:, rows] + sq1r[:, rows]) / d_model + 1e-5))
        cos_t, sin_t = cos_b[rows, :], sin_b[rows, :]
        q = ((qkeep[i].astype(F32) + qrecv[i, :, :256].astype(F32)) * r).astype(BF16)
        kv = ((qsend[i, :, 256:].astype(F32) + qrecv[i, :, 256:].astype(F32)) * r).astype(BF16)
        qs[...] = (rope(q.astype(F32), cos_t, sin_t).astype(F32) * 0.125).astype(BF16)
        k = rope(kv[:, :128].astype(F32), cos_t, sin_t)
        v = kv[:, 128:]
        kvn[rows, :128] = k
        kvn[rows, 128:] = v
        main = PAST_MAX + i * BLK
        kk[main:main + BLK, :] = jnp.where(own, k[:, :64], k[:, 64:])
        vv[main:main + BLK, :] = jnp.where(own, v[:, :64], v[:, 64:])
        col = lax.broadcasted_iota(jnp.int32, (1, main), 1)
        bias = jnp.where((col >= p_ref[0]) & (col < PAST_MAX), NEG, 0.0)
        causal = lax.broadcasted_iota(jnp.int32, (BLK, BLK), 1) <= lax.broadcasted_iota(jnp.int32, (BLK, BLK), 0)

        def pair(n, carry):
            lanes = pl.ds(pl.multiple_of(n * 128, 128), 128)
            qp = qs[:, lanes]
            done = []
            for s in range(2):
                qn = qp[:, s * 64:(s + 1) * 64]
                s_main = lax.dot_general(qn, kk[:main, :], NT, preferred_element_type=F32) + bias
                s_diag = jnp.where(causal, lax.dot_general(qn, kk[main:main + BLK, :], NT, preferred_element_type=F32), NEG)
                top = jnp.maximum(jnp.max(s_main, axis=1, keepdims=True), jnp.max(s_diag, axis=1, keepdims=True))
                e_main = jnp.exp(s_main - top)
                e_diag = jnp.exp(s_diag - top)
                inv = 1.0 / (jnp.sum(e_main, axis=1, keepdims=True) + jnp.sum(e_diag, axis=1, keepdims=True))
                o = jnp.dot((e_main * inv).astype(BF16), vv[:main, :], preferred_element_type=F32)
                o += jnp.dot((e_diag * inv).astype(BF16), vv[main:main + BLK, :], preferred_element_type=F32)
                done.append(o.astype(BF16))
            ob[i, :, lanes] = jnp.concatenate(done, axis=1)
            return carry
        lax.fori_loop(0, 2, pair, 0)
        o_copy(i).start()

    def wo_step(i):
        o_copy(i).wait_recv()
        acc[...] = jnp.dot(ob[i], wo[pl.ds(pl.multiple_of(h * 256, 256), 256), :], preferred_element_type=F32)
        acc[...] += jnp.dot(orecv[i], wo[pl.ds(pl.multiple_of((1 - h) * 256, 256), 256), :], preferred_element_type=F32)
        ckeep[i] = acc[pl.ds(pl.multiple_of(c * HALF, HALF), HALF), :].astype(BF16)
        csend[i] = acc[pl.ds(pl.multiple_of((1 - c) * HALF, HALF), HALF), :].astype(BF16)
        c_copy(i).start()

    def add(a, b):
        return (a.astype(F32) + b.astype(F32)).astype(BF16)

    def c_step(i):
        c_copy(i).wait_recv()
        part[i] = add(ckeep[i], crecv[i])
        x_copy(i).start()

    def x_step(i):
        x_copy(i).wait_recv()
        res = x[pl.ds(pl.multiple_of(i * BLK + c * HALF, HALF), HALF), :]
        mid[i, 0] = add(res, add(part[i], xrecv[i]))
        d_copy(i).start()

    def d_step(i):
        d_copy(i).wait_recv()
        for k in range(2):
            m = mid[i, k].astype(F32)
            sq2[i, :, k * HALF:(k + 1) * HALF] = row_sums(m)
            hg[k * HALF:(k + 1) * HALF, :] = (m * g2_ref[...]).astype(BF16)

    def gate_up(side, j, dst):
        cols = pl.ds(pl.multiple_of(side * (CH * CW) + j * CW, CW), CW)
        dst[:, :CW] = jnp.dot(hg[...], wg[:, cols], preferred_element_type=F32).astype(BF16)
        dst[:, CW:] = jnp.dot(hg[...], wu[:, cols], preferred_element_type=F32).astype(BF16)

    def u_step(i, j):
        gate_up(1 - h, j, gsend.at[i, j])
        g_copy(i, j).start()
        gate_up(h, j, gkeep.at[i % 2, j])

    def v_step(i, j):
        g_copy(i, j).wait_recv()
        r = as_column(lax.rsqrt((sq2[i] + sq2r[i]) / d_model + 1e-5))
        both = ((gkeep[i % 2, j].astype(F32) + grecv[i, j].astype(F32)) * r).astype(BF16).astype(F32)
        g, e = both[:, :CW], both[:, CW:]
        ab[i, j] = (g * jax.nn.sigmoid(g) * e).astype(BF16)
        a_copy(i, j).start()

    def w_step(i, j):
        a_copy(i, j).wait_recv()
        mine = wd[pl.ds(pl.multiple_of(h * (CH * CW) + j * CW, CW), CW), :]
        theirs = wd[pl.ds(pl.multiple_of((1 - h) * (CH * CW) + j * CW, CW), CW), :]
        y = jnp.dot(ab[i, j], mine, preferred_element_type=F32) + jnp.dot(arecv[i, j], theirs, preferred_element_type=F32)
        acc[...] = jnp.where(j == 0, 0.0, acc[...]) + y

    def e_start(i):
        ekeep[i] = acc[:HALF].astype(BF16)
        esend[i] = acc[HALF:].astype(BF16)
        e_copy(i).start()

    def e_step(i):
        e_copy(i).wait_recv()
        part2[i] = add(ekeep[i], erecv[i])
        y_copy(i).start()

    def y_step(i):
        y_copy(i).wait_recv()
        fin[i, 0] = add(mid[i, 0], add(part2[i], yrecv[i]))
        f_copy(i).start()

    def out_copy(i, k):
        at = pl.multiple_of(i * BLK + (c * HALF if k == 0 else (1 - c) * HALF), HALF)
        return pltpu.make_async_copy(fin.at[i, k], out_hbm.at[pl.ds(at, HALF), :], osem.at[2 * i + k])

    def f_step(i):
        out_copy(i, 0).start()
        f_copy(i).wait_recv()
        out_copy(i, 1).start()

    def loop(*steps):
        def body(j, carry):
            for step, i in steps:
                step(i, j)
            return carry
        lax.fori_loop(0, CH, body, 0)

    def cache_rows():
        def tile(n, carry):
            rows = pl.ds(pl.multiple_of(n * BLK, BLK), BLK)
            at = n * BLK - p_ref[0] + lax.broadcasted_iota(jnp.int32, (BLK, NB * BLK), 0)
            pick = jnp.where(at == lax.broadcasted_iota(jnp.int32, (BLK, NB * BLK), 1), 1.0, 0.0).astype(BF16)
            new = jnp.dot(pick, kvn[...], preferred_element_type=F32)
            where = n * BLK - p_ref[0] + lax.broadcasted_iota(jnp.int32, (BLK, 128), 0)
            fresh = (where >= 0) & (where < NB * BLK)
            kc[rows, :] = jnp.where(fresh, new[:, :128], kc[rows, :].astype(F32)).astype(BF16)
            vc[rows, :] = jnp.where(fresh, new[:, 128:], vc[rows, :].astype(F32)).astype(BF16)
            return carry
        lax.fori_loop(0, kc.shape[0] // BLK, tile, 0)

    for cp in ld_q:
        cp.wait()
    for i in range(NB):
        ld_x[i].wait()
        qkv(i)
        if i < 2:
            q_copy(i).start()
    r_copy().start()
    for i in range(NB):
        tables(i)
    ld_kc.wait()
    ld_vc.wait()
    kk[:PAST_MAX, :] = jnp.where(own, kc[:PAST_MAX, :64], kc[:PAST_MAX, 64:])
    vv[:PAST_MAX, :] = jnp.where(own, vc[:PAST_MAX, :64], vc[:PAST_MAX, 64:])
    r_copy().wait_recv()
    att(0)
    q_copy(2).start()
    att(1)
    q_copy(3).start()
    ld_wo.wait()
    wo_step(0)
    c_step(0)
    att(2)
    x_step(0)
    wo_step(1)
    d_step(0)
    for cp in ld_gu:
        cp.wait()
    t_copy(0).start()
    loop((u_step, 0))
    c_step(1)
    att(3)
    x_step(1)
    wo_step(2)
    d_step(1)
    t_copy(1).start()
    t_copy(0).wait_recv()
    c_step(2)
    loop((u_step, 1), (v_step, 0))
    x_step(2)
    wo_step(3)
    c_step(3)
    d_step(2)
    t_copy(2).start()
    t_copy(1).wait_recv()
    ld_wd.wait()
    loop((u_step, 2), (v_step, 1), (w_step, 0))
    e_start(0)
    x_step(3)
    d_step(3)
    t_copy(3).start()
    e_step(0)
    t_copy(2).wait_recv()
    cache_rows()
    ko = pltpu.make_async_copy(kc, ko_hbm, osem.at[8])
    vo = pltpu.make_async_copy(vc, vo_hbm, osem.at[9])
    ko.start()
    vo.start()
    loop((u_step, 3), (v_step, 2), (w_step, 1))
    e_start(1)
    y_step(0)
    e_step(1)
    f_step(0)
    t_copy(3).wait_recv()
    loop((v_step, 3), (w_step, 2))
    e_start(2)
    y_step(1)
    e_step(2)
    f_step(1)
    loop((w_step, 3))
    e_start(3)
    y_step(2)
    e_step(3)
    f_step(2)
    y_step(3)
    f_step(3)

    r_copy().wait_send()
    for i in range(NB):
        for cp in (q_copy, o_copy, c_copy, x_copy, d_copy, t_copy, e_copy, y_copy, f_copy):
            cp(i).wait_send()

        def drain(j, carry, i=i):
            g_copy(i, j).wait_send()
            a_copy(i, j).wait_send()
            return carry
        lax.fori_loop(0, CH, drain, 0)
        out_copy(i, 0).wait()
        out_copy(i, 1).wait()
    ko.wait()
    vo.wait()


def solution(mesh):
    def local_layer(hidden, rms_attn, rms_mlp, w_q, w_k, w_v, w_o, w_gate, w_up, w_down, k_cache, v_cache, past_len):
        new_len, width = hidden.shape
        freq = jnp.exp((jnp.arange(128) % 32).astype(F32) * (-2.0 * math.log(ROPE_BASE) / 64)).reshape(1, 128)
        k_flat = k_cache.reshape(-1, 128)
        v_flat = v_cache.reshape(-1, 128)
        any_spec = pl.BlockSpec(memory_space=pl.ANY)
        vmem_spec = pl.BlockSpec(memory_space=pltpu.VMEM)

        def v(*shape, dtype=BF16):
            return pltpu.VMEM(shape, dtype)
        tok = v(NB, HALF, width)
        scratch = [
            v(new_len, width), v(*w_q.shape), v(*w_k.shape), v(*w_v.shape), v(*w_o.shape), v(*w_gate.shape), v(*w_up.shape), v(*w_down.shape),
            v(*k_flat.shape), v(*v_flat.shape),
            v(NB, BLK, 512), v(NB, BLK, 256), v(NB, BLK, 512), v(8, new_len, dtype=F32), v(8, new_len, dtype=F32),
            v(new_len, 128, dtype=F32), v(new_len, 128, dtype=F32), v(PAST_MAX + new_len, 64), v(PAST_MAX + new_len, 64),
            v(BLK, 256), v(new_len, 256), v(NB, BLK, 256), v(NB, BLK, 256),
            tok, tok, tok, tok, tok, v(NB, 2, HALF, width), v(NB, 8, BLK, dtype=F32), v(NB, 8, BLK, dtype=F32), v(BLK, width),
            v(NB, CH, BLK, 2 * CW), v(2, CH, BLK, 2 * CW), v(NB, CH, BLK, 2 * CW), v(NB, CH, BLK, CW), v(NB, CH, BLK, CW),
            v(BLK, width, dtype=F32),
            tok, tok, tok, tok, tok, v(NB, 2, HALF, width),
            pltpu.SemaphoreType.DMA((13,)), pltpu.SemaphoreType.DMA((10,)),
            pltpu.SemaphoreType.DMA((N_REMOTE,)), pltpu.SemaphoreType.DMA((N_REMOTE,)),
        ]
        out, k_full, v_full = pl.pallas_call(
            lambda *refs: kernel(2 * width, *refs),
            out_shape=(jax.ShapeDtypeStruct((new_len, width), BF16), jax.ShapeDtypeStruct(k_flat.shape, BF16),
                       jax.ShapeDtypeStruct(v_flat.shape, BF16)),
            in_specs=[pl.BlockSpec(memory_space=pltpu.SMEM), any_spec, vmem_spec, vmem_spec, vmem_spec] + [any_spec] * 9,
            out_specs=(any_spec,) * 3,
            scratch_shapes=scratch,
            compiler_params=pltpu.CompilerParams(collective_id=0, has_side_effects=True, vmem_limit_bytes=67043328),
            name="layer",
        )(past_len, hidden, rms_attn.reshape(1, width), rms_mlp.reshape(1, width), freq, w_q, w_k, w_v, w_o, w_gate, w_up, w_down,
          k_flat, v_flat)
        return out, k_full.reshape(k_cache.shape), v_full.reshape(v_cache.shape)

    row_split = P('hid', 'tp')
    col_split = P('tp', 'hid')
    cache_spec = P('dp', 'tp', None)
    in_specs = (P('dp', 'hid'), P('hid'), P('hid'), row_split, row_split, row_split, col_split,
                row_split, row_split, col_split, cache_spec, cache_spec, P('dp'))
    out_specs = (P('dp', 'hid'), cache_spec, cache_spec)
    return jax.shard_map(local_layer, mesh=mesh, in_specs=in_specs, out_specs=out_specs, check_vma=False)
```

time: 471 us -> 208 us (0.44)
  waiting for transfers between devices: 327 us -> 0 us
  Pallas kernels: 0 us -> 195 us
  matrix products: 89.5 us -> 0 us
  between operations: 14.9 us -> 1.29 us
  other arithmetic: 12.8 us -> 0.52 us
  blocking collectives: 11.2 us -> 0 us
    psum x2 -> x0, waiting for transfers between devices: 236 us -> none  [the longest x1 192 us: local_layer(): gate_sum, up_sum = lax.psum((gate_part, up_part), 'hid')]
    pallas_call x0 -> x1, Pallas kernels: none -> 195 us  [local_layer(): pl.pallas_call(lambda *refs: kernel(2 * width, *refs), out_shape=(jax.Sha...]
    dot_general x8 -> x0, matrix products: 58.2 us -> none  [the longest x1 22.1 us: attend(): jnp.einsum('grct,tgd->cgrd', attn_probs, v_full, preferred_element_type=j...]
    reduce_scatter x2 -> x0, waiting for transfers between devices: 51.4 us -> none  [the longest x1 26 us: local_layer(): lax.psum_scatter(down_part, 'tp', scatter_dimension=0, tiled=True)]
    all_gather x2 -> x0, waiting for transfers between devices: 39.4 us -> none  [the longest x1 19.7 us: local_layer(): layer_out = lax.all_gather(out_rows, 'tp', axis=0, tiled=True)]
    sub x1 -> x0, matrix products: 31.4 us -> none  [attend(): jax.nn.softmax(jnp.where(causal, scores, -1e+30), axis=-1)]
    psum x2 -> x0, blocking collectives: 11.2 us -> none  [the longest x1 6.28 us: local_layer(): lax.psum(jnp.sum(hid_f32 * hid_f32, axis=1, keepdims=True), 'hid')]
    dynamic_update_slice x2 -> x0, local copies, waits for them, and re-layouts: 6.85 us -> none  [the longest x1 3.47 us: local_layer(): lax.dynamic_update_slice(v_cache, v_sum.reshape(new_len, kv_local, head_d...]
  transfers between devices with their start and end apart: 6 -> 0, of which waited for: 6 -> 0; matrix products, arithmetic and copies ran while one was open for 0% -> 0% of each run, Pallas kernels for 0% -> 0%
where the time goes in v1:
time: 208 us
  Pallas kernels  195 us (94%)
  local copies, waits for them, and re-layouts  11.2 us (5%)
    pallas_call x1, Pallas kernels, local_layer(): pl.pallas_call(lambda *refs: kernel(2 * width, *refs), out_shape=(jax.Sha...  195 us

profile of v1, /device:TPU:0, one launch (start us, length us, event | category | flops | bytes accessed | tf_op | source)
XLA Modules:
  0.0 208.0 jit_solution(9892918063301823680)
XLA Ops:
  1.3 0.5 fusion.2.refs_4_
  1.8 2.0 copy.20.refs_12_
  3.8 2.0 copy.21.refs_13_
  5.9 195.0 %layer.1 = (bf16[1024,1024]{1,0:T(8,128)(2,1)}, bf16[2048,128]{1,0:T(8,128)(2,1)}, bf16[2048,128]{1,0:T(8,128)(2,1)}) custom-call(s32[1]{0:T(128)S(6)} %copy.25.refs_0_, bf16[1024,1024]{1,0:T(8,128)(2,1)} %refs_1_.1, f32[1,1024]{1,0:T(1,128)} %bitcast.10, f32[1,1024]{1,0:T(1,128)} %bitcast.11, f32[1,128]{1,0:T(1,128)} %fusion.2.refs_4_, ...), custom_call_target="tpu_custom_call" | custom-call | tf_op jit(solution)/shard_map/layer/pallas_call | solution.py:368
  200.9 2.0 copy.22
  202.9 2.0 copy.23
  205.0 3.1 %copy.26 = bf16[1024,1024]{1,0:T(8,128)(2,1)} copy(bf16[1024,1024]{1,0:T(8,128)(2,1)} %get-tuple-element.15) | data formatting | bytes 4194304

commit v2 on v1

v2 whole, which is shorter than its diff:
```python
import math
import jax
import jax.numpy as jnp
from jax import lax
from jax.experimental import pallas as pl
from jax.experimental.pallas import tpu as pltpu
from jax.sharding import PartitionSpec as P

ROPE_BASE = 10000.0
F32, BF16 = jnp.float32, jnp.bfloat16
NEG = -1e30
BLK = 256
HALF = BLK // 2
PAST_MAX = 1024
NB = 4
CH = 4
CW = 256
MESH = pl.DeviceIdType.MESH

UNITS = ((0, 0, 256), (1, 0, 256), (2, 0, 256), (3, 0, 128), (3, 1, 128))
NU = len(UNITS)
Q, R, O, C, X, D, T = 0, 4, 5, 9, 13, 17, 21
E, Y, F, G = 25, 25 + NU, 25 + 2 * NU, 25 + 3 * NU
A = G + CH * NU
N_REMOTE = A + CH * NU


def rope(t, cos_t, sin_t):
    width = t.shape[1]
    lane = lax.broadcasted_iota(jnp.int32, t.shape, 1)
    swapped = jnp.where((lane & 63) < 32, pltpu.roll(t, width - 32, 1), pltpu.roll(t, 32, 1))
    cos_w = jnp.concatenate([cos_t] * (width // 128), axis=1)
    sin_w = jnp.concatenate([sin_t] * (width // 128), axis=1)
    return (t * cos_w + swapped * sin_w).astype(BF16)


def row_sums(t):
    sq = jnp.broadcast_to(jnp.sum(t * t, axis=1, keepdims=True), (t.shape[0], 128))
    return jnp.transpose(sq)[:8]


def as_column(row):
    return jnp.transpose(jnp.broadcast_to(row[:1], (128, row.shape[1])))[:, :1]


def kernel(d_model, p_ref, x_hbm, g1_ref, g2_ref, wq_hbm, wk_hbm, wv_hbm, wo_hbm, wg_hbm, wu_hbm, wd_hbm, kc_hbm, vc_hbm,
           out_hbm, ko_hbm, vo_hbm,
           x, wq, wk, wv, wo, wg, wu, wd, kc, vc, qsend, qkeep, qrecv, sq1, sq1r, cos_b, sin_b, kt, vv, qs, kvn, ob, orecv,
           csend, ckeep, crecv, part, xrecv, mid, sq2, sq2r, hg, sums, gsend, gkeep, grecv, ab, arecv, acc,
           esend, ekeep, erecv, part2, yrecv, fin, lsem, osem, ssem, rsem):
    h = lax.axis_index('hid')
    t = lax.axis_index('tp')
    c = lax.rem(t, 2)
    hid_dev = {'hid': 1 - h}
    core_dev = {'tp': t + 1 - 2 * c}
    x_dev = {'tp': lax.rem(t + 2, 4)}
    own = h == 0

    loads = []

    def load(src, dst):
        n = len(loads)
        cp = pltpu.make_async_copy(src, dst, lsem.at[n])
        cp.start()
        loads.append(cp)
        return cp

    ld_q = [load(wq_hbm, wq), load(wk_hbm, wk), load(wv_hbm, wv)]
    ld_x = [load(x_hbm.at[pl.ds(i * BLK, BLK)], x.at[pl.ds(i * BLK, BLK)]) for i in range(2)]

    barrier = pltpu.get_barrier_semaphore()
    for dev in (hid_dev, core_dev, x_dev):
        pl.semaphore_signal(barrier, inc=1, device_id=dev, device_id_type=MESH)
    pl.semaphore_wait(barrier, 3)

    def remote(src, dst, n, dev):
        return pltpu.make_async_remote_copy(src_ref=src, dst_ref=dst, send_sem=ssem.at[n], recv_sem=rsem.at[n],
                                            device_id=dev, device_id_type=MESH)

    def q_copy(i): return remote(qsend.at[i], qrecv.at[i], Q + i, hid_dev)
    def r_copy(): return remote(sq1, sq1r, R, hid_dev)
    def o_copy(i): return remote(ob.at[i], orecv.at[i], O + i, hid_dev)
    def c_copy(i): return remote(csend.at[i], crecv.at[i], C + i, core_dev)
    def x_copy(i): return remote(part.at[i], xrecv.at[i], X + i, x_dev)
    def d_copy(i): return remote(mid.at[i, 0], mid.at[i, 1], D + i, core_dev)
    def t_copy(i): return remote(sq2.at[i], sq2r.at[i], T + i, hid_dev)

    def whole(u):
        return pl.ds(UNITS[u][1] * UNITS[u][2], UNITS[u][2])

    def half(u):
        return pl.ds(UNITS[u][1] * UNITS[u][2] // 2, UNITS[u][2] // 2)

    def g_copy(u, j): return remote(gsend.at[UNITS[u][0], j, whole(u)], grecv.at[UNITS[u][0], j, whole(u)], G + CH * u + j, hid_dev)
    def a_copy(u, j): return remote(ab.at[UNITS[u][0], j, whole(u)], arecv.at[UNITS[u][0], j, whole(u)], A + CH * u + j, hid_dev)
    def e_copy(u): return remote(esend.at[UNITS[u][0], half(u)], erecv.at[UNITS[u][0], half(u)], E + u, core_dev)
    def y_copy(u): return remote(part2.at[UNITS[u][0], half(u)], yrecv.at[UNITS[u][0], half(u)], Y + u, x_dev)
    def f_copy(u): return remote(fin.at[UNITS[u][0], 0, half(u)], fin.at[UNITS[u][0], 1, half(u)], F + u, core_dev)

    def qkv(i, send):
        xf = x[pl.ds(i * BLK, BLK), :].astype(F32)
        xg = (xf * g1_ref[...]).astype(BF16)
        theirs = wq[:, pl.ds(pl.multiple_of((1 - h) * 256, 256), 256)]
        qsend[i, :, :256] = jnp.dot(xg, theirs, preferred_element_type=F32).astype(BF16)
        qsend[i, :, 256:384] = jnp.dot(xg, wk[...], preferred_element_type=F32).astype(BF16)
        qsend[i, :, 384:] = jnp.dot(xg, wv[...], preferred_element_type=F32).astype(BF16)
        if send:
            q_copy(i).start()
        mine = wq[:, pl.ds(pl.multiple_of(h * 256, 256), 256)]
        qkeep[i] = jnp.dot(xg, mine, preferred_element_type=F32).astype(BF16)
        sq1[:, i * BLK:(i + 1) * BLK] = row_sums(xf)

    def tables(i):
        pos = (p_ref[0] + i * BLK + lax.broadcasted_iota(jnp.int32, (BLK, 128), 0)).astype(F32)
        lane = lax.broadcasted_iota(jnp.int32, (BLK, 128), 1)
        freq = jnp.exp((lane[:8] & 31).astype(F32) * (-2.0 * math.log(ROPE_BASE) / 64))[:1]
        ang = pos * freq
        cos_b[pl.ds(i * BLK, BLK), :] = jnp.cos(ang)
        sin = jnp.sin(ang)
        sin_b[pl.ds(i * BLK, BLK), :] = jnp.where((lane & 63) < 32, -sin, sin)

    def att(i):
        rows = slice(i * BLK, (i + 1) * BLK)
        q_copy(i).wait_recv()
        r = as_column(lax.rsqrt((sq1[:, rows] + sq1r[:, rows]) / d_model + 1e-5))
        cos_t, sin_t = cos_b[rows, :], sin_b[rows, :]
        q = ((qkeep[i].astype(F32) + qrecv[i, :, :256].astype(F32)) * r).astype(BF16)
        kv = ((qsend[i, :, 256:].astype(F32) + qrecv[i, :, 256:].astype(F32)) * r).astype(BF16)
        qs[...] = (rope(q.astype(F32), cos_t, sin_t).astype(F32) * 0.125).astype(BF16)
        k = rope(kv[:, :128].astype(F32), cos_t, sin_t)
        v = kv[:, 128:]
        k_t = jnp.transpose(k.astype(F32)).astype(BF16)
        kvn[:128, rows] = k_t
        kvn[128:, rows] = jnp.transpose(v.astype(F32)).astype(BF16)
        main = PAST_MAX + i * BLK
        kt[:, main:main + BLK] = jnp.where(own, k_t[:64], k_t[64:])
        vv[main:main + BLK, :] = jnp.where(own, v[:, :64], v[:, 64:])
        col = lax.broadcasted_iota(jnp.int32, (1, main), 1)
        bias = jnp.where((col >= p_ref[0]) & (col < PAST_MAX), NEG, 0.0)
        causal = lax.broadcasted_iota(jnp.int32, (BLK, BLK), 1) <= lax.broadcasted_iota(jnp.int32, (BLK, BLK), 0)

        def pair(n, carry):
            lanes = pl.ds(pl.multiple_of(n * 128, 128), 128)
            qp = qs[:, lanes]
            done = []
            for s in range(2):
                qn = qp[:, s * 64:(s + 1) * 64]
                s_main = jnp.dot(qn, kt[:, :main], preferred_element_type=F32) + bias
                s_diag = jnp.where(causal, jnp.dot(qn, kt[:, main:main + BLK], preferred_element_type=F32), NEG)
                top = jnp.maximum(jnp.max(s_main, axis=1, keepdims=True), jnp.max(s_diag, axis=1, keepdims=True))
                e_main = jnp.exp(s_main - top)
                e_diag = jnp.exp(s_diag - top)
                inv = 1.0 / (jnp.sum(e_main, axis=1, keepdims=True) + jnp.sum(e_diag, axis=1, keepdims=True))
                o = jnp.dot((e_main * inv).astype(BF16), vv[:main, :], preferred_element_type=F32)
                o += jnp.dot((e_diag * inv).astype(BF16), vv[main:main + BLK, :], preferred_element_type=F32)
                done.append(o.astype(BF16))
            ob[i, :, lanes] = jnp.concatenate(done, axis=1)
            return carry
        lax.fori_loop(0, 2, pair, 0)
        o_copy(i).start()

    def wo_step(i):
        o_copy(i).wait_recv()
        acc[...] = jnp.dot(ob[i], wo[pl.ds(pl.multiple_of(h * 256, 256), 256), :], preferred_element_type=F32)
        acc[...] += jnp.dot(orecv[i], wo[pl.ds(pl.multiple_of((1 - h) * 256, 256), 256), :], preferred_element_type=F32)
        ckeep[i] = acc[pl.ds(pl.multiple_of(c * HALF, HALF), HALF), :].astype(BF16)
        csend[i] = acc[pl.ds(pl.multiple_of((1 - c) * HALF, HALF), HALF), :].astype(BF16)
        c_copy(i).start()

    def add(a, b):
        return (a.astype(F32) + b.astype(F32)).astype(BF16)

    def c_step(i):
        c_copy(i).wait_recv()
        part[i] = add(ckeep[i], crecv[i])
        x_copy(i).start()

    def x_step(i):
        x_copy(i).wait_recv()
        res = x[pl.ds(pl.multiple_of(i * BLK + c * HALF, HALF), HALF), :]
        mid[i, 0] = add(res, add(part[i], xrecv[i]))
        d_copy(i).start()

    def d_step(i):
        d_copy(i).wait_recv()
        at = 0
        for u in range(NU):
            if UNITS[u][0] != i:
                continue
            for k in range(2):
                n = UNITS[u][2] // 2
                m = mid[i, k, half(u), :].astype(F32)
                sq = jnp.broadcast_to(jnp.sum(m * m, axis=1, keepdims=True), (n, 128))
                sums[at:at + n, :] = sq
                hg[at:at + n, :] = (m * g2_ref[...]).astype(BF16)
                at += n
        sq2[i] = jnp.transpose(sums[...])[:8]

    def gate_up(u, side, j, dst):
        cols = pl.ds(pl.multiple_of(side * (CH * CW) + j * CW, CW), CW)
        rows = hg[whole(u), :]
        dst[:, :CW] = jnp.dot(rows, wg[:, cols], preferred_element_type=F32).astype(BF16)
        dst[:, CW:] = jnp.dot(rows, wu[:, cols], preferred_element_type=F32).astype(BF16)

    def u_step(u, j):
        i = UNITS[u][0]
        gate_up(u, 1 - h, j, gsend.at[i, j, whole(u)])
        g_copy(u, j).start()
        gate_up(u, h, j, gkeep.at[i % 2, j, whole(u)])

    def v_step(u, j):
        i = UNITS[u][0]
        g_copy(u, j).wait_recv()
        r = as_column(lax.rsqrt((sq2[i, :, whole(u)] + sq2r[i, :, whole(u)]) / d_model + 1e-5))
        both = ((gkeep[i % 2, j, whole(u), :].astype(F32) + grecv[i, j, whole(u), :].astype(F32)) * r).astype(BF16).astype(F32)
        g, e = both[:, :CW], both[:, CW:]
        ab[i, j, whole(u), :] = (g * jax.nn.sigmoid(g) * e).astype(BF16)
        a_copy(u, j).start()

    def w_step(u, j):
        i = UNITS[u][0]
        a_copy(u, j).wait_recv()
        mine = wd[pl.ds(pl.multiple_of(h * (CH * CW) + j * CW, CW), CW), :]
        theirs = wd[pl.ds(pl.multiple_of((1 - h) * (CH * CW) + j * CW, CW), CW), :]
        y = jnp.dot(ab[i, j, whole(u), :], mine, preferred_element_type=F32)
        y += jnp.dot(arecv[i, j, whole(u), :], theirs, preferred_element_type=F32)
        acc[whole(u), :] = jnp.where(j == 0, 0.0, acc[whole(u), :]) + y

    def e_start(u):
        i, k, n = UNITS[u]
        ekeep[i, half(u), :] = acc[k * n:k * n + n // 2, :].astype(BF16)
        esend[i, half(u), :] = acc[k * n + n // 2:k * n + n, :].astype(BF16)
        e_copy(u).start()

    def e_step(u):
        i = UNITS[u][0]
        e_copy(u).wait_recv()
        part2[i, half(u), :] = add(ekeep[i, half(u), :], erecv[i, half(u), :])
        y_copy(u).start()

    def y_step(u):
        i = UNITS[u][0]
        y_copy(u).wait_recv()
        down = add(part2[i, half(u), :], yrecv[i, half(u), :])
        fin[i, 0, half(u), :] = add(mid[i, 0, half(u), :], down)
        f_copy(u).start()

    def out_copy(u, k):
        i, part_no, n = UNITS[u]
        at = pl.multiple_of(i * BLK + (c if k == 0 else 1 - c) * HALF + part_no * (n // 2), 64)
        return pltpu.make_async_copy(fin.at[i, k, half(u)], out_hbm.at[pl.ds(at, n // 2), :], osem.at[2 * u + k])

    def f_step(u):
        out_copy(u, 0).start()
        f_copy(u).wait_recv()
        out_copy(u, 1).start()

    def loop(*steps):
        def body(j, carry):
            for step, i in steps:
                step(i, j)
            return carry
        lax.fori_loop(0, CH, body, 0)

    def cache_rows():
        def tile(n, carry):
            cols = pl.ds(pl.multiple_of(n * BLK, BLK), BLK)
            at = n * BLK - p_ref[0] + lax.broadcasted_iota(jnp.int32, (NB * BLK, BLK), 1)
            pick = jnp.where(at == lax.broadcasted_iota(jnp.int32, (NB * BLK, BLK), 0), 1.0, 0.0).astype(BF16)
            new = jnp.dot(kvn[...], pick, preferred_element_type=F32)
            where = n * BLK - p_ref[0] + lax.broadcasted_iota(jnp.int32, (128, BLK), 1)
            fresh = (where >= 0) & (where < NB * BLK)
            kc[:, cols] = jnp.where(fresh, new[:128], kc[:, cols].astype(F32)).astype(BF16)
            vc[:, cols] = jnp.where(fresh, new[128:], vc[:, cols].astype(F32)).astype(BF16)
            return carry
        lax.fori_loop(0, kc.shape[1] // BLK, tile, 0)

    for cp in ld_q:
        cp.wait()
    ld_x[0].wait()
    qkv(0, True)
    ld_x += [load(x_hbm.at[pl.ds(i * BLK, BLK)], x.at[pl.ds(i * BLK, BLK)]) for i in range(2, NB)]
    ld_kc, ld_vc = load(kc_hbm, kc), load(vc_hbm, vc)
    ld_wo = load(wo_hbm, wo)
    ld_gu = [load(wg_hbm, wg), load(wu_hbm, wu)]
    ld_wd = load(wd_hbm, wd)
    for i in range(1, NB):
        ld_x[i].wait()
        qkv(i, i < 2)
    r_copy().start()
    for i in range(NB):
        tables(i)
    ld_kc.wait()
    ld_vc.wait()
    kt[:, :PAST_MAX] = kc[pl.ds(pl.multiple_of(h * 64, 64), 64), :PAST_MAX]
    v_old = jnp.transpose(vc[:, :PAST_MAX].astype(F32)).astype(BF16)
    vv[:PAST_MAX, :] = jnp.where(own, v_old[:, :64], v_old[:, 64:])
    r_copy().wait_recv()
    att(0)
    q_copy(2).start()
    att(1)
    q_copy(3).start()
    ld_wo.wait()
    wo_step(0)
    c_step(0)
    att(2)
    x_step(0)
    wo_step(1)
    d_step(0)
    for cp in ld_gu:
        cp.wait()
    t_copy(0).start()
    loop((u_step, 0))
    c_step(1)
    att(3)
    x_step(1)
    wo_step(2)
    d_step(1)
    t_copy(1).start()
    t_copy(0).wait_recv()
    c_step(2)
    loop((u_step, 1), (v_step, 0))
    x_step(2)
    wo_step(3)
    c_step(3)
    d_step(2)
    t_copy(2).start()
    t_copy(1).wait_recv()
    ld_wd.wait()
    loop((u_step, 2), (v_step, 1), (w_step, 0))
    e_start(0)
    x_step(3)
    d_step(3)
    t_copy(3).start()
    e_step(0)
    t_copy(2).wait_recv()
    cache_rows()
    ko = pltpu.make_async_copy(kc, ko_hbm, osem.at[2 * NU])
    vo = pltpu.make_async_copy(vc, vo_hbm, osem.at[2 * NU + 1])
    ko.start()
    vo.start()
    loop((u_step, 3), (v_step, 2), (w_step, 1))
    loop((u_step, 4))
    e_start(1)
    y_step(0)
    e_step(1)
    f_step(0)
    t_copy(3).wait_recv()
    loop((v_step, 3), (w_step, 2))
    e_start(2)
    y_step(1)
    e_step(2)
    f_step(1)
    loop((v_step, 4))
    y_step(2)
    loop((w_step, 3))
    e_start(3)
    f_step(2)
    w_step(4, 0)
    e_step(3)
    for j in range(1, CH):
        w_step(4, j)
    e_start(4)
    y_step(3)
    e_step(4)
    f_step(3)
    y_step(4)
    f_step(4)

    r_copy().wait_send()
    for i in range(NB):
        for cp in (q_copy, o_copy, c_copy, x_copy, d_copy, t_copy):
            cp(i).wait_send()
    for u in range(NU):
        for cp in (e_copy, y_copy, f_copy):
            cp(u).wait_send()

        def drain(j, carry, u=u):
            g_copy(u, j).wait_send()
            a_copy(u, j).wait_send()
            return carry
        lax.fori_loop(0, CH, drain, 0)
        out_copy(u, 0).wait()
        out_copy(u, 1).wait()
    ko.wait()
    vo.wait()


def results_body(pieces, *refs):
    n = len(pieces)
    srcs, dsts, bufs, isem, osem = refs[:3], refs[3:6], refs[6:9], refs[9], refs[10]

    def read(k):
        a, start, size = pieces[k]
        part = pl.ds(start, size)
        return pltpu.make_async_copy(srcs[a].at[part], bufs[a].at[part], isem.at[k])

    def write(k):
        a, start, size = pieces[k]
        part = pl.ds(start, size)
        return pltpu.make_async_copy(bufs[a].at[part], dsts[a].at[part], osem.at[k])
    for k in range(n):
        read(k).start()
    for k in range(n):
        read(k).wait()
        write(k).start()
    for k in range(n):
        write(k).wait()


def solution(mesh):
    def local_layer(hidden, rms_attn, rms_mlp, w_q, w_k, w_v, w_o, w_gate, w_up, w_down, k_cache, v_cache, past_len):
        new_len, width = hidden.shape
        tokens = k_cache.shape[0]
        k_flat = k_cache.transpose(1, 2, 0).reshape(-1, tokens)
        v_flat = v_cache.transpose(1, 2, 0).reshape(-1, tokens)
        any_spec = pl.BlockSpec(memory_space=pl.ANY)
        vmem_spec = pl.BlockSpec(memory_space=pltpu.VMEM)

        def v(*shape, dtype=BF16):
            return pltpu.VMEM(shape, dtype)
        tok = v(NB, HALF, width)
        scratch = [
            v(new_len, width), v(*w_q.shape), v(*w_k.shape), v(*w_v.shape), v(*w_o.shape), v(*w_gate.shape), v(*w_up.shape), v(*w_down.shape),
            v(*k_flat.shape), v(*v_flat.shape),
            v(NB, BLK, 512), v(NB, BLK, 256), v(NB, BLK, 512), v(8, new_len, dtype=F32), v(8, new_len, dtype=F32),
            v(new_len, 128, dtype=F32), v(new_len, 128, dtype=F32), v(64, PAST_MAX + new_len), v(PAST_MAX + new_len, 64),
            v(BLK, 256), v(256, new_len), v(NB, BLK, 256), v(NB, BLK, 256),
            tok, tok, tok, tok, tok, v(NB, 2, HALF, width), v(NB, 8, BLK, dtype=F32), v(NB, 8, BLK, dtype=F32), v(BLK, width), v(BLK, 128, dtype=F32),
            v(NB, CH, BLK, 2 * CW), v(2, CH, BLK, 2 * CW), v(NB, CH, BLK, 2 * CW), v(NB, CH, BLK, CW), v(NB, CH, BLK, CW),
            v(BLK, width, dtype=F32),
            tok, tok, tok, tok, tok, v(NB, 2, HALF, width),
            pltpu.SemaphoreType.DMA((13,)), pltpu.SemaphoreType.DMA((2 * NU + 2,)),
            pltpu.SemaphoreType.DMA((N_REMOTE,)), pltpu.SemaphoreType.DMA((N_REMOTE,)),
        ]
        shapes = tuple(jax.ShapeDtypeStruct(a, BF16) for a in (hidden.shape, k_flat.shape, v_flat.shape))
        done = pl.pallas_call(
            lambda *refs: kernel(2 * width, *refs),
            out_shape=shapes,
            in_specs=[pl.BlockSpec(memory_space=pltpu.SMEM), any_spec, vmem_spec, vmem_spec] + [any_spec] * 9,
            out_specs=(any_spec,) * 3,
            scratch_shapes=scratch,
            compiler_params=pltpu.CompilerParams(collective_id=0, has_side_effects=True, vmem_limit_bytes=67043328),
            name="layer",
        )(past_len, hidden, rms_attn.reshape(1, width), rms_mlp.reshape(1, width), w_q, w_k, w_v, w_o, w_gate, w_up, w_down,
          k_flat, v_flat)
        pieces = [(0, k * 128, 128) for k in range(new_len // 128)] + [(a, k * 64, 64) for a in (1, 2) for k in range(2)]
        out, k_full, v_full = pl.pallas_call(
            lambda *refs: results_body(pieces, *refs),
            out_shape=shapes, in_specs=[any_spec] * 3, out_specs=(any_spec,) * 3,
            scratch_shapes=[v(*a.shape) for a in shapes] + [pltpu.SemaphoreType.DMA((len(pieces),))] * 2,
            compiler_params=pltpu.CompilerParams(vmem_limit_bytes=60 << 20),
            name="results",
        )(*done)
        heads, dim = k_cache.shape[1:]
        return (out, k_full.reshape(heads, dim, tokens).transpose(2, 0, 1), v_full.reshape(heads, dim, tokens).transpose(2, 0, 1))

    row_split = P('hid', 'tp')
    col_split = P('tp', 'hid')
    cache_spec = P('dp', 'tp', None)
    in_specs = (P('dp', 'hid'), P('hid'), P('hid'), row_split, row_split, row_split, col_split,
                row_split, row_split, col_split, cache_spec, cache_spec, P('dp'))
    out_specs = (P('dp', 'hid'), cache_spec, cache_spec)
    return jax.shard_map(local_layer, mesh=mesh, in_specs=in_specs, out_specs=out_specs, check_vma=False)
```

time: 208 us -> 196 us (0.942)
  local copies, waits for them, and re-layouts: 11.2 us -> 0 us
    pallas_call x2 -> x0, local copies, waits for them, and re-layouts: 4.08 us -> none  [local_layer(): pl.pallas_call(lambda *refs: kernel(2 * width, *refs), out_shape=(jax.Sha...]
    reshape x2 -> x0, local copies, waits for them, and re-layouts: 4.08 us -> none  [the longest x1 2.04 us: local_layer(): k_flat = k_cache.reshape(-1, 128)]
    unnamed x1 -> x0, local copies, waits for them, and re-layouts: 3.08 us -> none
    pallas_call x1 -> x2, Pallas kernels: 195 us -> 194 us  [the longest x1 191 us: local_layer(): pl.pallas_call(lambda *refs: kernel(2 * width, *refs), out_shape=shapes,...]
where the time goes in v2:
time: 196 us
  Pallas kernels  194 us (99%)
    pallas_call x1, Pallas kernels, local_layer(): pl.pallas_call(lambda *refs: kernel(2 * width, *refs), out_shape=shapes,...  191 us

profile of v2, /device:TPU:0, one launch (start us, length us, event | category | flops | bytes accessed | tf_op | source)
XLA Modules:
  0.0 195.8 jit_solution(2256067421759745892)
XLA Ops:
  1.3 191.5 %layer.1 = (bf16[1024,1024]{1,0:T(8,128)(2,1)}, bf16[128,2048]{1,0:T(8,128)(2,1)}, bf16[128,2048]{1,0:T(8,128)(2,1)}) custom-call(s32[1]{0:T(128)S(6)} %copy.16.refs_0_, bf16[1024,1024]{1,0:T(8,128)(2,1)} %refs_1_.1, f32[1,1024]{1,0:T(1,128)} %bitcast.16, f32[1,1024]{1,0:T(1,128)} %bitcast.17, bf16[1024,512]{1,0:T(8,128)(2,1)} %refs_4_.1, ...), custom_call_target="tpu_custom_call" | custom-call | tf_op jit(solution)/shard_map/layer/pallas_call | solution.py:437
  192.8 2.8 %results.1 = (bf16[1024,1024]{1,0:T(8,128)(2,1)}, bf16[128,2048]{1,0:T(8,128)(2,1)}, bf16[128,2048]{1,0:T(8,128)(2,1)}) custom-call(bf16[1024,1024]{1,0:T(8,128)(2,1)} %get-tuple-element.9.refs_0_, bf16[128,2048]{1,0:T(8,128)(2,1)} %get-tuple-element.10.refs_1_, bf16[128,2048]{1,0:T(8,128)(2,1)} %get-tuple-element.11.refs_2_), custom_call_target="tpu_custom_call" | custom-call | tf_op jit(solution)/shard_map/results/pallas_call | solution.py:448

commit v3 on v2

--- a/solution.py
+++ b/solution.py
@@ -19,8 +19,8 @@
 
 UNITS = ((0, 0, 256), (1, 0, 256), (2, 0, 256), (3, 0, 128), (3, 1, 128))
 NU = len(UNITS)
-Q, R, O, C, X, D, T = 0, 4, 5, 9, 13, 17, 21
-E, Y, F, G = 25, 25 + NU, 25 + 2 * NU, 25 + 3 * NU
+Q, R, O, C, X, D, T = 0, 4, 8, 12, 16, 20, 24
+E, Y, F, G = 28, 28 + NU, 28 + 2 * NU, 28 + 3 * NU
 A = G + CH * NU
 N_REMOTE = A + CH * NU
 
@@ -43,9 +43,9 @@
     return jnp.transpose(jnp.broadcast_to(row[:1], (128, row.shape[1])))[:, :1]
 
 
-def kernel(d_model, p_ref, x_hbm, g1_ref, g2_ref, wq_hbm, wk_hbm, wv_hbm, wo_hbm, wg_hbm, wu_hbm, wd_hbm, kc_hbm, vc_hbm,
+def kernel(d_model, p_hbm, x_hbm, g1_hbm, g2_hbm, wq_hbm, wk_hbm, wv_hbm, wo_hbm, wg_hbm, wu_hbm, wd_hbm, kc_hbm, vc_hbm,
            out_hbm, ko_hbm, vo_hbm,
-           x, wq, wk, wv, wo, wg, wu, wd, kc, vc, qsend, qkeep, qrecv, sq1, sq1r, cos_b, sin_b, kt, vv, qs, kvn, ob, orecv,
+           p_ref, g1_ref, g2_ref, x, wq, wk, wv, wo, wg, wu, wd, kc, vc, qsend, qkeep, qrecv, sq1, sq1r, cos_b, sin_b, kt, vv, qs, kvn, ob, orecv,
            csend, ckeep, crecv, part, xrecv, mid, sq2, sq2r, hg, sums, gsend, gkeep, grecv, ab, arecv, acc,
            esend, ekeep, erecv, part2, yrecv, fin, lsem, osem, ssem, rsem):
     h = lax.axis_index('hid')
@@ -65,8 +65,10 @@
         loads.append(cp)
         return cp
 
-    ld_q = [load(wq_hbm, wq), load(wk_hbm, wk), load(wv_hbm, wv)]
-    ld_x = [load(x_hbm.at[pl.ds(i * BLK, BLK)], x.at[pl.ds(i * BLK, BLK)]) for i in range(2)]
+    ld_x = [load(x_hbm.at[pl.ds(0, BLK)], x.at[pl.ds(0, BLK)])]
+    ld_q = [load(g1_hbm, g1_ref), load(wq_hbm, wq), load(wk_hbm, wk), load(wv_hbm, wv)]
+    ld_x += [load(x_hbm.at[pl.ds(BLK, BLK)], x.at[pl.ds(BLK, BLK)])]
+    ld_small = [load(p_hbm, p_ref), load(g2_hbm, g2_ref)]
 
     barrier = pltpu.get_barrier_semaphore()
     for dev in (hid_dev, core_dev, x_dev):
@@ -78,7 +80,7 @@
                                             device_id=dev, device_id_type=MESH)
 
     def q_copy(i): return remote(qsend.at[i], qrecv.at[i], Q + i, hid_dev)
-    def r_copy(): return remote(sq1, sq1r, R, hid_dev)
+    def r_copy(i): return remote(sq1.at[i], sq1r.at[i], R + i, hid_dev)
     def o_copy(i): return remote(ob.at[i], orecv.at[i], O + i, hid_dev)
     def c_copy(i): return remote(csend.at[i], crecv.at[i], C + i, core_dev)
     def x_copy(i): return remote(part.at[i], xrecv.at[i], X + i, x_dev)
@@ -108,7 +110,9 @@
             q_copy(i).start()
         mine = wq[:, pl.ds(pl.multiple_of(h * 256, 256), 256)]
         qkeep[i] = jnp.dot(xg, mine, preferred_element_type=F32).astype(BF16)
-        sq1[:, i * BLK:(i + 1) * BLK] = row_sums(xf)
+        sq1[i] = row_sums(xf)
+        if send:
+            r_copy(i).start()
 
     def tables(i):
         pos = (p_ref[0] + i * BLK + lax.broadcasted_iota(jnp.int32, (BLK, 128), 0)).astype(F32)
@@ -122,7 +126,8 @@
     def att(i):
         rows = slice(i * BLK, (i + 1) * BLK)
         q_copy(i).wait_recv()
-        r = as_column(lax.rsqrt((sq1[:, rows] + sq1r[:, rows]) / d_model + 1e-5))
+        r_copy(i).wait_recv()
+        r = as_column(lax.rsqrt((sq1[i] + sq1r[i]) / d_model + 1e-5))
         cos_t, sin_t = cos_b[rows, :], sin_b[rows, :]
         q = ((qkeep[i].astype(F32) + qrecv[i, :, :256].astype(F32)) * r).astype(BF16)
         kv = ((qsend[i, :, 256:].astype(F32) + qrecv[i, :, 256:].astype(F32)) * r).astype(BF16)
@@ -287,7 +292,8 @@
     for i in range(1, NB):
         ld_x[i].wait()
         qkv(i, i < 2)
-    r_copy().start()
+    for cp in ld_small:
+        cp.wait()
     for i in range(NB):
         tables(i)
     ld_kc.wait()
@@ -295,11 +301,12 @@
     kt[:, :PAST_MAX] = kc[pl.ds(pl.multiple_of(h * 64, 64), 64), :PAST_MAX]
     v_old = jnp.transpose(vc[:, :PAST_MAX].astype(F32)).astype(BF16)
     vv[:PAST_MAX, :] = jnp.where(own, v_old[:, :64], v_old[:, 64:])
-    r_copy().wait_recv()
     att(0)
     q_copy(2).start()
+    r_copy(2).start()
     att(1)
     q_copy(3).start()
+    r_copy(3).start()
     ld_wo.wait()
     wo_step(0)
     c_step(0)
@@ -367,9 +374,8 @@
     y_step(4)
     f_step(4)
 
-    r_copy().wait_send()
     for i in range(NB):
-        for cp in (q_copy, o_copy, c_copy, x_copy, d_copy, t_copy):
+        for cp in (q_copy, r_copy, o_copy, c_copy, x_copy, d_copy, t_copy):
             cp(i).wait_send()
     for u in range(NU):
         for cp in (e_copy, y_copy, f_copy):
@@ -415,29 +421,29 @@
         k_flat = k_cache.transpose(1, 2, 0).reshape(-1, tokens)
         v_flat = v_cache.transpose(1, 2, 0).reshape(-1, tokens)
         any_spec = pl.BlockSpec(memory_space=pl.ANY)
-        vmem_spec = pl.BlockSpec(memory_space=pltpu.VMEM)
 
         def v(*shape, dtype=BF16):
             return pltpu.VMEM(shape, dtype)
         tok = v(NB, HALF, width)
         scratch = [
+            pltpu.SMEM((1,), jnp.int32), v(1, width, dtype=F32), v(1, width, dtype=F32),
             v(new_len, width), v(*w_q.shape), v(*w_k.shape), v(*w_v.shape), v(*w_o.shape), v(*w_gate.shape), v(*w_up.shape), v(*w_down.shape),
             v(*k_flat.shape), v(*v_flat.shape),
-            v(NB, BLK, 512), v(NB, BLK, 256), v(NB, BLK, 512), v(8, new_len, dtype=F32), v(8, new_len, dtype=F32),
+            v(NB, BLK, 512), v(NB, BLK, 256), v(NB, BLK, 512), v(NB, 8, BLK, dtype=F32), v(NB, 8, BLK, dtype=F32),
             v(new_len, 128, dtype=F32), v(new_len, 128, dtype=F32), v(64, PAST_MAX + new_len), v(PAST_MAX + new_len, 64),
             v(BLK, 256), v(256, new_len), v(NB, BLK, 256), v(NB, BLK, 256),
             tok, tok, tok, tok, tok, v(NB, 2, HALF, width), v(NB, 8, BLK, dtype=F32), v(NB, 8, BLK, dtype=F32), v(BLK, width), v(BLK, 128, dtype=F32),
             v(NB, CH, BLK, 2 * CW), v(2, CH, BLK, 2 * CW), v(NB, CH, BLK, 2 * CW), v(NB, CH, BLK, CW), v(NB, CH, BLK, CW),
             v(BLK, width, dtype=F32),
             tok, tok, tok, tok, tok, v(NB, 2, HALF, width),
-            pltpu.SemaphoreType.DMA((13,)), pltpu.SemaphoreType.DMA((2 * NU + 2,)),
+            pltpu.SemaphoreType.DMA((16,)), pltpu.SemaphoreType.DMA((2 * NU + 2,)),
             pltpu.SemaphoreType.DMA((N_REMOTE,)), pltpu.SemaphoreType.DMA((N_REMOTE,)),
         ]
         shapes = tuple(jax.ShapeDtypeStruct(a, BF16) for a in (hidden.shape, k_flat.shape, v_flat.shape))
         done = pl.pallas_call(
             lambda *refs: kernel(2 * width, *refs),
             out_shape=shapes,
-            in_specs=[pl.BlockSpec(memory_space=pltpu.SMEM), any_spec, vmem_spec, vmem_spec] + [any_spec] * 9,
+            in_specs=[any_spec] * 13,
             out_specs=(any_spec,) * 3,
             scratch_shapes=scratch,
             compiler_params=pltpu.CompilerParams(collective_id=0, has_side_effects=True, vmem_limit_bytes=67043328),

time: 196 us -> 191 us (0.974)
  Pallas kernels: 194 us -> 189 us
    pallas_call x1, Pallas kernels: 191 us -> 186 us  [local_layer(): pl.pallas_call(lambda *refs: kernel(2 * width, *refs), out_shape=shapes,...]
where the time goes in v3:
time: 191 us; the launch traced here: 190 us
  Pallas kernels  189 us (99%)
    pallas_call x1, Pallas kernels, local_layer(): pl.pallas_call(lambda *refs: kernel(2 * width, *refs), out_shape=shapes,...  186 us

profile of v3, /device:TPU:0, one launch (start us, length us, event | category | flops | bytes accessed | tf_op | source)
XLA Modules:
  0.0 190.5 jit_solution(8788963796514199061)
XLA Ops:
  1.3 186.2 %layer.1 = (bf16[1024,1024]{1,0:T(8,128)(2,1)}, bf16[128,2048]{1,0:T(8,128)(2,1)}, bf16[128,2048]{1,0:T(8,128)(2,1)}) custom-call(s32[1]{0:T(128)S(6)} %copy.16.refs_0_, bf16[1024,1024]{1,0:T(8,128)(2,1)} %refs_1_.1, f32[1,1024]{1,0:T(1,128)} %bitcast.16, f32[1,1024]{1,0:T(1,128)} %bitcast.17, bf16[1024,512]{1,0:T(8,128)(2,1)} %refs_4_.1, ...), custom_call_target="tpu_custom_call" | custom-call | tf_op jit(solution)/shard_map/layer/pallas_call | solution.py:443
  187.5 2.8 %results.1 = (bf16[1024,1024]{1,0:T(8,128)(2,1)}, bf16[128,2048]{1,0:T(8,128)(2,1)}, bf16[128,2048]{1,0:T(8,128)(2,1)}) custom-call(bf16[1024,1024]{1,0:T(8,128)(2,1)} %get-tuple-element.9.refs_0_, bf16[128,2048]{1,0:T(8,128)(2,1)} %get-tuple-element.10.refs_1_, bf16[128,2048]{1,0:T(8,128)(2,1)} %get-tuple-element.11.refs_2_), custom_call_target="tpu_custom_call" | custom-call | tf_op jit(solution)/shard_map/results/pallas_call | solution.py:454

commit v4 on v3

--- a/solution.py
+++ b/solution.py
@@ -17,7 +17,7 @@
 CW = 256
 MESH = pl.DeviceIdType.MESH
 
-UNITS = ((0, 0, 256), (1, 0, 256), (2, 0, 256), (3, 0, 128), (3, 1, 128))
+UNITS = ((0, 0, 256), (1, 0, 256), (2, 0, 256), (3, 0, 128), (3, 2, 64), (3, 3, 64))
 NU = len(UNITS)
 Q, R, O, C, X, D, T = 0, 4, 8, 12, 16, 20, 24
 E, Y, F, G = 28, 28 + NU, 28 + 2 * NU, 28 + 3 * NU
@@ -44,10 +44,10 @@
 
 
 def kernel(d_model, p_hbm, x_hbm, g1_hbm, g2_hbm, wq_hbm, wk_hbm, wv_hbm, wo_hbm, wg_hbm, wu_hbm, wd_hbm, kc_hbm, vc_hbm,
-           out_hbm, ko_hbm, vo_hbm,
-           p_ref, g1_ref, g2_ref, x, wq, wk, wv, wo, wg, wu, wd, kc, vc, qsend, qkeep, qrecv, sq1, sq1r, cos_b, sin_b, kt, vv, qs, kvn, ob, orecv,
+           fin, kc, vc,
+           p_ref, g1_ref, g2_ref, x, wq, wk, wv, wo, wg, wu, wd, qsend, qkeep, qrecv, sq1, sq1r, cos_b, sin_b, kt, vv, qs, kvn, ob, orecv,
            csend, ckeep, crecv, part, xrecv, mid, sq2, sq2r, hg, sums, gsend, gkeep, grecv, ab, arecv, acc,
-           esend, ekeep, erecv, part2, yrecv, fin, lsem, osem, ssem, rsem):
+           esend, ekeep, erecv, part2, yrecv, lsem, ssem, rsem):
     h = lax.axis_index('hid')
     t = lax.axis_index('tp')
     c = lax.rem(t, 2)
@@ -73,7 +73,6 @@
     barrier = pltpu.get_barrier_semaphore()
     for dev in (hid_dev, core_dev, x_dev):
         pl.semaphore_signal(barrier, inc=1, device_id=dev, device_id_type=MESH)
-    pl.semaphore_wait(barrier, 3)
 
     def remote(src, dst, n, dev):
         return pltpu.make_async_remote_copy(src_ref=src, dst_ref=dst, send_sem=ssem.at[n], recv_sem=rsem.at[n],
@@ -106,6 +105,8 @@
         qsend[i, :, :256] = jnp.dot(xg, theirs, preferred_element_type=F32).astype(BF16)
         qsend[i, :, 256:384] = jnp.dot(xg, wk[...], preferred_element_type=F32).astype(BF16)
         qsend[i, :, 384:] = jnp.dot(xg, wv[...], preferred_element_type=F32).astype(BF16)
+        if i == 0:
+            pl.semaphore_wait(barrier, 3)
         if send:
             q_copy(i).start()
         mine = wq[:, pl.ds(pl.multiple_of(h * 256, 256), 256)]
@@ -216,7 +217,7 @@
     def v_step(u, j):
         i = UNITS[u][0]
         g_copy(u, j).wait_recv()
-        r = as_column(lax.rsqrt((sq2[i, :, whole(u)] + sq2r[i, :, whole(u)]) / d_model + 1e-5))
+        r = as_column(lax.rsqrt((sq2[i] + sq2r[i]) / d_model + 1e-5))[UNITS[u][1] * UNITS[u][2]:(UNITS[u][1] + 1) * UNITS[u][2]]
         both = ((gkeep[i % 2, j, whole(u), :].astype(F32) + grecv[i, j, whole(u), :].astype(F32)) * r).astype(BF16).astype(F32)
         g, e = both[:, :CW], both[:, CW:]
         ab[i, j, whole(u), :] = (g * jax.nn.sigmoid(g) * e).astype(BF16)
@@ -250,15 +251,8 @@
         fin[i, 0, half(u), :] = add(mid[i, 0, half(u), :], down)
         f_copy(u).start()
 
-    def out_copy(u, k):
-        i, part_no, n = UNITS[u]
-        at = pl.multiple_of(i * BLK + (c if k == 0 else 1 - c) * HALF + part_no * (n // 2), 64)
-        return pltpu.make_async_copy(fin.at[i, k, half(u)], out_hbm.at[pl.ds(at, n // 2), :], osem.at[2 * u + k])
-
     def f_step(u):
-        out_copy(u, 0).start()
         f_copy(u).wait_recv()
-        out_copy(u, 1).start()
 
     def loop(*steps):
         def body(j, carry):
@@ -342,12 +336,9 @@
     e_step(0)
     t_copy(2).wait_recv()
     cache_rows()
-    ko = pltpu.make_async_copy(kc, ko_hbm, osem.at[2 * NU])
-    vo = pltpu.make_async_copy(vc, vo_hbm, osem.at[2 * NU + 1])
-    ko.start()
-    vo.start()
     loop((u_step, 3), (v_step, 2), (w_step, 1))
     loop((u_step, 4))
+    loop((u_step, 5))
     e_start(1)
     y_step(0)
     e_step(1)
@@ -359,6 +350,7 @@
     e_step(2)
     f_step(1)
     loop((v_step, 4))
+    loop((v_step, 5))
     y_step(2)
     loop((w_step, 3))
     e_start(3)
@@ -368,11 +360,18 @@
     for j in range(1, CH):
         w_step(4, j)
     e_start(4)
+    w_step(5, 0)
+    e_step(4)
+    for j in range(1, CH):
+        w_step(5, j)
+    e_start(5)
     y_step(3)
-    e_step(4)
+    e_step(5)
+    y_step(4)
     f_step(3)
-    y_step(4)
+    y_step(5)
     f_step(4)
+    f_step(5)
 
     for i in range(NB):
         for cp in (q_copy, r_copy, o_copy, c_copy, x_copy, d_copy, t_copy):
@@ -386,32 +385,19 @@
             a_copy(u, j).wait_send()
             return carry
         lax.fori_loop(0, CH, drain, 0)
-        out_copy(u, 0).wait()
-        out_copy(u, 1).wait()
-    ko.wait()
-    vo.wait()
-
-
-def results_body(pieces, *refs):
-    n = len(pieces)
-    srcs, dsts, bufs, isem, osem = refs[:3], refs[3:6], refs[6:9], refs[9], refs[10]
-
-    def read(k):
-        a, start, size = pieces[k]
-        part = pl.ds(start, size)
-        return pltpu.make_async_copy(srcs[a].at[part], bufs[a].at[part], isem.at[k])
-
-    def write(k):
-        a, start, size = pieces[k]
-        part = pl.ds(start, size)
-        return pltpu.make_async_copy(bufs[a].at[part], dsts[a].at[part], osem.at[k])
-    for k in range(n):
-        read(k).start()
-    for k in range(n):
-        read(k).wait()
-        write(k).start()
-    for k in range(n):
-        write(k).wait()
+
+
+def results_body(fin, kc, vc, out_hbm, ko_hbm, vo_hbm, sem):
+    c = lax.rem(lax.axis_index('tp'), 2)
+    copies = [pltpu.make_async_copy(kc, ko_hbm, sem.at[2 * NB]), pltpu.make_async_copy(vc, vo_hbm, sem.at[2 * NB + 1])]
+    for i in range(NB):
+        for k in range(2):
+            at = pl.multiple_of(i * BLK + (c if k == 0 else 1 - c) * HALF, HALF)
+            copies.append(pltpu.make_async_copy(fin.at[i, k], out_hbm.at[pl.ds(at, HALF)], sem.at[2 * i + k]))
+    for cp in copies:
+        cp.start()
+    for cp in copies:
+        cp.wait()
 
 
 def solution(mesh):
@@ -428,34 +414,34 @@
         scratch = [
             pltpu.SMEM((1,), jnp.int32), v(1, width, dtype=F32), v(1, width, dtype=F32),
             v(new_len, width), v(*w_q.shape), v(*w_k.shape), v(*w_v.shape), v(*w_o.shape), v(*w_gate.shape), v(*w_up.shape), v(*w_down.shape),
-            v(*k_flat.shape), v(*v_flat.shape),
             v(NB, BLK, 512), v(NB, BLK, 256), v(NB, BLK, 512), v(NB, 8, BLK, dtype=F32), v(NB, 8, BLK, dtype=F32),
             v(new_len, 128, dtype=F32), v(new_len, 128, dtype=F32), v(64, PAST_MAX + new_len), v(PAST_MAX + new_len, 64),
             v(BLK, 256), v(256, new_len), v(NB, BLK, 256), v(NB, BLK, 256),
             tok, tok, tok, tok, tok, v(NB, 2, HALF, width), v(NB, 8, BLK, dtype=F32), v(NB, 8, BLK, dtype=F32), v(BLK, width), v(BLK, 128, dtype=F32),
             v(NB, CH, BLK, 2 * CW), v(2, CH, BLK, 2 * CW), v(NB, CH, BLK, 2 * CW), v(NB, CH, BLK, CW), v(NB, CH, BLK, CW),
             v(BLK, width, dtype=F32),
-            tok, tok, tok, tok, tok, v(NB, 2, HALF, width),
-            pltpu.SemaphoreType.DMA((16,)), pltpu.SemaphoreType.DMA((2 * NU + 2,)),
+            tok, tok, tok, tok, tok,
+            pltpu.SemaphoreType.DMA((16,)),
             pltpu.SemaphoreType.DMA((N_REMOTE,)), pltpu.SemaphoreType.DMA((N_REMOTE,)),
         ]
-        shapes = tuple(jax.ShapeDtypeStruct(a, BF16) for a in (hidden.shape, k_flat.shape, v_flat.shape))
+        kept = ((NB, 2, HALF, width), k_flat.shape, v_flat.shape)
+        vmem_spec = pl.BlockSpec(memory_space=pltpu.VMEM)
         done = pl.pallas_call(
             lambda *refs: kernel(2 * width, *refs),
-            out_shape=shapes,
+            out_shape=tuple(v(*a) for a in kept),
             in_specs=[any_spec] * 13,
-            out_specs=(any_spec,) * 3,
+            out_specs=(vmem_spec,) * 3,
             scratch_shapes=scratch,
-            compiler_params=pltpu.CompilerParams(collective_id=0, has_side_effects=True, vmem_limit_bytes=67043328),
+            compiler_params=pltpu.CompilerParams(collective_id=0, has_side_effects=True, vmem_limit_bytes=60 << 20),
             name="layer",
         )(past_len, hidden, rms_attn.reshape(1, width), rms_mlp.reshape(1, width), w_q, w_k, w_v, w_o, w_gate, w_up, w_down,
           k_flat, v_flat)
-        pieces = [(0, k * 128, 128) for k in range(new_len // 128)] + [(a, k * 64, 64) for a in (1, 2) for k in range(2)]
         out, k_full, v_full = pl.pallas_call(
-            lambda *refs: results_body(pieces, *refs),
-            out_shape=shapes, in_specs=[any_spec] * 3, out_specs=(any_spec,) * 3,
-            scratch_shapes=[v(*a.shape) for a in shapes] + [pltpu.SemaphoreType.DMA((len(pieces),))] * 2,
-            compiler_params=pltpu.CompilerParams(vmem_limit_bytes=60 << 20),
+            results_body,
+            out_shape=tuple(jax.ShapeDtypeStruct(a, BF16) for a in (hidden.shape, k_flat.shape, v_flat.shape)),
+            in_specs=[vmem_spec] * 3, out_specs=(any_spec,) * 3,
+            scratch_shapes=[pltpu.SemaphoreType.DMA((2 * NB + 2,))],
+            compiler_params=pltpu.CompilerParams(vmem_limit_bytes=1 << 20),
             name="results",
         )(*done)
         heads, dim = k_cache.shape[1:]

time: 191 us -> 188 us (0.984)
  Pallas kernels: 189 us -> 186 us
    pallas_call x2, Pallas kernels: 189 us -> 186 us  [the longest x1 184 us: local_layer(): pl.pallas_call(lambda *refs: kernel(2 * width, *refs), out_shape=tuple((v...]
where the time goes in v4:
time: 188 us; the launch traced here: 187 us
  Pallas kernels  186 us (99%)
    pallas_call x1, Pallas kernels, local_layer(): pl.pallas_call(lambda *refs: kernel(2 * width, *refs), out_shape=tuple((v...  184 us

profile of v4, /device:TPU:0, one launch (start us, length us, event | category | flops | bytes accessed | tf_op | source)
XLA Modules:
  0.0 187.5 jit_solution(1502094427046000040)
XLA Ops:
  1.3 184.3 %layer.1 = (bf16[4,2,128,1024]{3,2,1,0:T(8,128)(2,1)S(1)}, bf16[128,2048]{1,0:T(8,128)(2,1)S(1)}, bf16[128,2048]{1,0:T(8,128)(2,1)S(1)}) custom-call(s32[1]{0:T(128)S(6)} %copy.16.refs_0_, bf16[1024,1024]{1,0:T(8,128)(2,1)} %refs_1_.1, f32[1,1024]{1,0:T(1,128)} %bitcast.16, f32[1,1024]{1,0:T(1,128)} %bitcast.17, bf16[1024,512]{1,0:T(8,128)(2,1)} %refs_4_.1, ...), custom_call_target="tpu_custom_call" | custom-call | tf_op jit(solution)/shard_map/layer/pallas_call | solution.py:429
  185.6 1.7 results.1

commit v5 on v4

--- a/solution.py
+++ b/solution.py
@@ -22,7 +22,8 @@
 Q, R, O, C, X, D, T = 0, 4, 8, 12, 16, 20, 24
 E, Y, F, G = 28, 28 + NU, 28 + 2 * NU, 28 + 3 * NU
 A = G + CH * NU
-N_REMOTE = A + CH * NU
+KV = A + CH * NU
+N_REMOTE = KV + NB
 
 
 def rope(t, cos_t, sin_t):
@@ -45,7 +46,7 @@
 
 def kernel(d_model, p_hbm, x_hbm, g1_hbm, g2_hbm, wq_hbm, wk_hbm, wv_hbm, wo_hbm, wg_hbm, wu_hbm, wd_hbm, kc_hbm, vc_hbm,
            fin, kc, vc,
-           p_ref, g1_ref, g2_ref, x, wq, wk, wv, wo, wg, wu, wd, qsend, qkeep, qrecv, sq1, sq1r, cos_b, sin_b, kt, vv, qs, kvn, ob, orecv,
+           p_ref, g1_ref, g2_ref, x, wq, wk, wv, wo, wg, wu, wd, qsend, qkeep, qrecv, sq1, sq1r, cos_b, sin_b, kt, vv, qs, kvn, kvsend, kvrecv, ob, orecv,
            csend, ckeep, crecv, part, xrecv, mid, sq2, sq2r, hg, sums, gsend, gkeep, grecv, ab, arecv, acc,
            esend, ekeep, erecv, part2, yrecv, lsem, ssem, rsem):
     h = lax.axis_index('hid')
@@ -81,6 +82,7 @@
     def q_copy(i): return remote(qsend.at[i], qrecv.at[i], Q + i, hid_dev)
     def r_copy(i): return remote(sq1.at[i], sq1r.at[i], R + i, hid_dev)
     def o_copy(i): return remote(ob.at[i], orecv.at[i], O + i, hid_dev)
+    def kv_copy(i): return remote(kvsend.at[i], kvrecv.at[i], KV + i, hid_dev)
     def c_copy(i): return remote(csend.at[i], crecv.at[i], C + i, core_dev)
     def x_copy(i): return remote(part.at[i], xrecv.at[i], X + i, x_dev)
     def d_copy(i): return remote(mid.at[i, 0], mid.at[i, 1], D + i, core_dev)
@@ -103,12 +105,16 @@
         xg = (xf * g1_ref[...]).astype(BF16)
         theirs = wq[:, pl.ds(pl.multiple_of((1 - h) * 256, 256), 256)]
         qsend[i, :, :256] = jnp.dot(xg, theirs, preferred_element_type=F32).astype(BF16)
-        qsend[i, :, 256:384] = jnp.dot(xg, wk[...], preferred_element_type=F32).astype(BF16)
-        qsend[i, :, 384:] = jnp.dot(xg, wv[...], preferred_element_type=F32).astype(BF16)
+        k = jnp.dot(xg, wk[...], preferred_element_type=F32).astype(BF16)
+        v = jnp.dot(xg, wv[...], preferred_element_type=F32).astype(BF16)
+        low = jnp.concatenate([k[:, :64], v[:, :64]], axis=1)
+        high = jnp.concatenate([k[:, 64:], v[:, 64:]], axis=1)
+        qsend[i, :, 256:] = jnp.where(own, high, low)
         if i == 0:
             pl.semaphore_wait(barrier, 3)
         if send:
             q_copy(i).start()
+        kvsend[i] = jnp.where(own, low, high)
         mine = wq[:, pl.ds(pl.multiple_of(h * 256, 256), 256)]
         qkeep[i] = jnp.dot(xg, mine, preferred_element_type=F32).astype(BF16)
         sq1[i] = row_sums(xf)
@@ -124,23 +130,29 @@
         sin = jnp.sin(ang)
         sin_b[pl.ds(i * BLK, BLK), :] = jnp.where((lane & 63) < 32, -sin, sin)
 
+    def row_factor(i):
+        return as_column(lax.rsqrt((sq1[i] + sq1r[i]) / d_model + 1e-5))
+
+    def keys_values(i, r, mine, theirs):
+        rows = slice(i * BLK, (i + 1) * BLK)
+        kv = ((mine.astype(F32) + theirs.astype(F32)) * r).astype(BF16)
+        lane = lax.broadcasted_iota(jnp.int32, kv.shape, 1)
+        return jnp.where(lane < 64, rope(kv.astype(F32), cos_b[rows, :], sin_b[rows, :]), kv)
+
     def att(i):
         rows = slice(i * BLK, (i + 1) * BLK)
         q_copy(i).wait_recv()
         r_copy(i).wait_recv()
-        r = as_column(lax.rsqrt((sq1[i] + sq1r[i]) / d_model + 1e-5))
+        r = row_factor(i)
         cos_t, sin_t = cos_b[rows, :], sin_b[rows, :]
         q = ((qkeep[i].astype(F32) + qrecv[i, :, :256].astype(F32)) * r).astype(BF16)
-        kv = ((qsend[i, :, 256:].astype(F32) + qrecv[i, :, 256:].astype(F32)) * r).astype(BF16)
+        kv = keys_values(i, r, kvsend[i], qrecv[i, :, 256:])
         qs[...] = (rope(q.astype(F32), cos_t, sin_t).astype(F32) * 0.125).astype(BF16)
-        k = rope(kv[:, :128].astype(F32), cos_t, sin_t)
-        v = kv[:, 128:]
-        k_t = jnp.transpose(k.astype(F32)).astype(BF16)
-        kvn[:128, rows] = k_t
-        kvn[128:, rows] = jnp.transpose(v.astype(F32)).astype(BF16)
+        kv_t = jnp.transpose(kv.astype(F32)).astype(BF16)
+        kvn[i] = kv_t
         main = PAST_MAX + i * BLK
-        kt[:, main:main + BLK] = jnp.where(own, k_t[:64], k_t[64:])
-        vv[main:main + BLK, :] = jnp.where(own, v[:, :64], v[:, 64:])
+        kt[:, main:main + BLK] = kv_t[:64]
+        vv[main:main + BLK, :] = kv[:, 64:]
         col = lax.broadcasted_iota(jnp.int32, (1, main), 1)
         bias = jnp.where((col >= p_ref[0]) & (col < PAST_MAX), NEG, 0.0)
         causal = lax.broadcasted_iota(jnp.int32, (BLK, BLK), 1) <= lax.broadcasted_iota(jnp.int32, (BLK, BLK), 0)
@@ -261,18 +273,26 @@
             return carry
         lax.fori_loop(0, CH, body, 0)
 
-    def cache_rows():
+    def place(i, head, kv_t):
+        lanes = pl.ds(pl.multiple_of(head * 64, 64), 64)
+
         def tile(n, carry):
             cols = pl.ds(pl.multiple_of(n * BLK, BLK), BLK)
-            at = n * BLK - p_ref[0] + lax.broadcasted_iota(jnp.int32, (NB * BLK, BLK), 1)
-            pick = jnp.where(at == lax.broadcasted_iota(jnp.int32, (NB * BLK, BLK), 0), 1.0, 0.0).astype(BF16)
-            new = jnp.dot(kvn[...], pick, preferred_element_type=F32)
-            where = n * BLK - p_ref[0] + lax.broadcasted_iota(jnp.int32, (128, BLK), 1)
-            fresh = (where >= 0) & (where < NB * BLK)
-            kc[:, cols] = jnp.where(fresh, new[:128], kc[:, cols].astype(F32)).astype(BF16)
-            vc[:, cols] = jnp.where(fresh, new[128:], vc[:, cols].astype(F32)).astype(BF16)
+            first = (n - i) * BLK - p_ref[0]
+            at = first + lax.broadcasted_iota(jnp.int32, (BLK, BLK), 1)
+            pick = jnp.where(at == lax.broadcasted_iota(jnp.int32, (BLK, BLK), 0), 1.0, 0.0).astype(BF16)
+            new = jnp.dot(kv_t, pick, preferred_element_type=F32)
+            where = first + lax.broadcasted_iota(jnp.int32, (64, BLK), 1)
+            fresh = (where >= 0) & (where < BLK)
+            kc[lanes, cols] = jnp.where(fresh, new[:64], kc[lanes, cols].astype(F32)).astype(BF16)
+            vc[lanes, cols] = jnp.where(fresh, new[64:], vc[lanes, cols].astype(F32)).astype(BF16)
             return carry
-        lax.fori_loop(0, kc.shape[1] // BLK, tile, 0)
+        lax.fori_loop(i + 1, i + 1 + PAST_MAX // BLK, tile, 0)
+
+    def kv_step(i):
+        kv_copy(i).wait_recv()
+        kv = keys_values(i, row_factor(i), qsend[i, :, 256:], kvrecv[i])
+        place(i, 1 - h, jnp.transpose(kv.astype(F32)).astype(BF16))
 
     for cp in ld_q:
         cp.wait()
@@ -335,7 +355,8 @@
     t_copy(3).start()
     e_step(0)
     t_copy(2).wait_recv()
-    cache_rows()
+    for i in range(NB):
+        place(i, h, kvn[i])
     loop((u_step, 3), (v_step, 2), (w_step, 1))
     loop((u_step, 4))
     loop((u_step, 5))
@@ -351,6 +372,8 @@
     f_step(1)
     loop((v_step, 4))
     loop((v_step, 5))
+    for i in range(NB):
+        kv_copy(i).start()
     y_step(2)
     loop((w_step, 3))
     e_start(3)
@@ -367,14 +390,18 @@
     e_start(5)
     y_step(3)
     e_step(5)
+    kv_step(0)
     y_step(4)
     f_step(3)
+    kv_step(1)
+    kv_step(2)
     y_step(5)
     f_step(4)
+    kv_step(3)
     f_step(5)
 
     for i in range(NB):
-        for cp in (q_copy, r_copy, o_copy, c_copy, x_copy, d_copy, t_copy):
+        for cp in (q_copy, r_copy, kv_copy, o_copy, c_copy, x_copy, d_copy, t_copy):
             cp(i).wait_send()
     for u in range(NU):
         for cp in (e_copy, y_copy, f_copy):
@@ -414,9 +441,9 @@
         scratch = [
             pltpu.SMEM((1,), jnp.int32), v(1, width, dtype=F32), v(1, width, dtype=F32),
             v(new_len, width), v(*w_q.shape), v(*w_k.shape), v(*w_v.shape), v(*w_o.shape), v(*w_gate.shape), v(*w_up.shape), v(*w_down.shape),
-            v(NB, BLK, 512), v(NB, BLK, 256), v(NB, BLK, 512), v(NB, 8, BLK, dtype=F32), v(NB, 8, BLK, dtype=F32),
+            v(NB, BLK, 384), v(NB, BLK, 256), v(NB, BLK, 384), v(NB, 8, BLK, dtype=F32), v(NB, 8, BLK, dtype=F32),
             v(new_len, 128, dtype=F32), v(new_len, 128, dtype=F32), v(64, PAST_MAX + new_len), v(PAST_MAX + new_len, 64),
-            v(BLK, 256), v(256, new_len), v(NB, BLK, 256), v(NB, BLK, 256),
+            v(BLK, 256), v(NB, 128, BLK), v(NB, BLK, 128), v(NB, BLK, 128), v(NB, BLK, 256), v(NB, BLK, 256),
             tok, tok, tok, tok, tok, v(NB, 2, HALF, width), v(NB, 8, BLK, dtype=F32), v(NB, 8, BLK, dtype=F32), v(BLK, width), v(BLK, 128, dtype=F32),
             v(NB, CH, BLK, 2 * CW), v(2, CH, BLK, 2 * CW), v(NB, CH, BLK, 2 * CW), v(NB, CH, BLK, CW), v(NB, CH, BLK, CW),
             v(BLK, width, dtype=F32),

time: 188 us -> 185 us (0.984)
  Pallas kernels: 186 us -> 183 us
    pallas_call x1, Pallas kernels: 184 us -> 181 us  [local_layer(): pl.pallas_call(lambda *refs: kernel(2 * width, *refs), out_shape=tuple((v...]
where the time goes in v5:
time: 185 us
  Pallas kernels  183 us (99%)
    pallas_call x1, Pallas kernels, local_layer(): pl.pallas_call(lambda *refs: kernel(2 * width, *refs), out_shape=tuple((v...  181 us

profile of v5, /device:TPU:0, one launch (start us, length us, event | category | flops | bytes accessed | tf_op | source)
XLA Modules:
  0.0 184.6 jit_solution(5279613421214751561)
XLA Ops:
  1.3 181.4 %layer.1 = (bf16[4,2,128,1024]{3,2,1,0:T(8,128)(2,1)S(1)}, bf16[128,2048]{1,0:T(8,128)(2,1)S(1)}, bf16[128,2048]{1,0:T(8,128)(2,1)S(1)}) custom-call(s32[1]{0:T(128)S(6)} %copy.16.refs_0_, bf16[1024,1024]{1,0:T(8,128)(2,1)} %refs_1_.1, f32[1,1024]{1,0:T(1,128)} %bitcast.16, f32[1,1024]{1,0:T(1,128)} %bitcast.17, bf16[1024,512]{1,0:T(8,128)(2,1)} %refs_4_.1, ...), custom_call_target="tpu_custom_call" | custom-call | tf_op jit(solution)/shard_map/layer/pallas_call | solution.py:456
  182.7 1.7 results.1

commit v6 on v5

--- a/solution.py
+++ b/solution.py
@@ -19,8 +19,8 @@
 
 UNITS = ((0, 0, 256), (1, 0, 256), (2, 0, 256), (3, 0, 128), (3, 2, 64), (3, 3, 64))
 NU = len(UNITS)
-Q, R, O, C, X, D, T = 0, 4, 8, 12, 16, 20, 24
-E, Y, F, G = 28, 28 + NU, 28 + 2 * NU, 28 + 3 * NU
+Q, R, C, X, D, T, O = 0, 4, 8, 12, 16, 20, 24
+E, Y, F, G = 32, 32 + NU, 32 + 2 * NU, 32 + 3 * NU
 A = G + CH * NU
 KV = A + CH * NU
 N_REMOTE = KV + NB
@@ -81,7 +81,7 @@
 
     def q_copy(i): return remote(qsend.at[i], qrecv.at[i], Q + i, hid_dev)
     def r_copy(i): return remote(sq1.at[i], sq1r.at[i], R + i, hid_dev)
-    def o_copy(i): return remote(ob.at[i], orecv.at[i], O + i, hid_dev)
+    def o_copy(i, n): return remote(ob.at[i, n], orecv.at[i, n], O + 2 * i + n, hid_dev)
     def kv_copy(i): return remote(kvsend.at[i], kvrecv.at[i], KV + i, hid_dev)
     def c_copy(i): return remote(csend.at[i], crecv.at[i], C + i, core_dev)
     def x_copy(i): return remote(part.at[i], xrecv.at[i], X + i, x_dev)
@@ -172,15 +172,18 @@
                 o = jnp.dot((e_main * inv).astype(BF16), vv[:main, :], preferred_element_type=F32)
                 o += jnp.dot((e_diag * inv).astype(BF16), vv[main:main + BLK, :], preferred_element_type=F32)
                 done.append(o.astype(BF16))
-            ob[i, :, lanes] = jnp.concatenate(done, axis=1)
+            ob[i, n] = jnp.concatenate(done, axis=1)
+            o_copy(i, n).start()
             return carry
         lax.fori_loop(0, 2, pair, 0)
-        o_copy(i).start()
 
     def wo_step(i):
-        o_copy(i).wait_recv()
-        acc[...] = jnp.dot(ob[i], wo[pl.ds(pl.multiple_of(h * 256, 256), 256), :], preferred_element_type=F32)
-        acc[...] += jnp.dot(orecv[i], wo[pl.ds(pl.multiple_of((1 - h) * 256, 256), 256), :], preferred_element_type=F32)
+        o_copy(i, 0).wait_recv()
+        o_copy(i, 1).wait_recv()
+        mine = jnp.concatenate([ob[i, 0], ob[i, 1]], axis=1)
+        theirs = jnp.concatenate([orecv[i, 0], orecv[i, 1]], axis=1)
+        acc[...] = jnp.dot(mine, wo[pl.ds(pl.multiple_of(h * 256, 256), 256), :], preferred_element_type=F32)
+        acc[...] += jnp.dot(theirs, wo[pl.ds(pl.multiple_of((1 - h) * 256, 256), 256), :], preferred_element_type=F32)
         ckeep[i] = acc[pl.ds(pl.multiple_of(c * HALF, HALF), HALF), :].astype(BF16)
         csend[i] = acc[pl.ds(pl.multiple_of((1 - c) * HALF, HALF), HALF), :].astype(BF16)
         c_copy(i).start()
@@ -401,8 +404,10 @@
     f_step(5)
 
     for i in range(NB):
-        for cp in (q_copy, r_copy, kv_copy, o_copy, c_copy, x_copy, d_copy, t_copy):
+        for cp in (q_copy, r_copy, kv_copy, c_copy, x_copy, d_copy, t_copy):
             cp(i).wait_send()
+        for n in range(2):
+            o_copy(i, n).wait_send()
     for u in range(NU):
         for cp in (e_copy, y_copy, f_copy):
             cp(u).wait_send()
@@ -443,7 +448,7 @@
             v(new_len, width), v(*w_q.shape), v(*w_k.shape), v(*w_v.shape), v(*w_o.shape), v(*w_gate.shape), v(*w_up.shape), v(*w_down.shape),
             v(NB, BLK, 384), v(NB, BLK, 256), v(NB, BLK, 384), v(NB, 8, BLK, dtype=F32), v(NB, 8, BLK, dtype=F32),
             v(new_len, 128, dtype=F32), v(new_len, 128, dtype=F32), v(64, PAST_MAX + new_len), v(PAST_MAX + new_len, 64),
-            v(BLK, 256), v(NB, 128, BLK), v(NB, BLK, 128), v(NB, BLK, 128), v(NB, BLK, 256), v(NB, BLK, 256),
+            v(BLK, 256), v(NB, 128, BLK), v(NB, BLK, 128), v(NB, BLK, 128), v(NB, 2, BLK, 128), v(NB, 2, BLK, 128),
             tok, tok, tok, tok, tok, v(NB, 2, HALF, width), v(NB, 8, BLK, dtype=F32), v(NB, 8, BLK, dtype=F32), v(BLK, width), v(BLK, 128, dtype=F32),
             v(NB, CH, BLK, 2 * CW), v(2, CH, BLK, 2 * CW), v(NB, CH, BLK, 2 * CW), v(NB, CH, BLK, CW), v(NB, CH, BLK, CW),
             v(BLK, width, dtype=F32),

time: 185 us -> 183 us (0.989)
  no operation moved by 1% of the time
where the time goes in v6:
time: 183 us
  Pallas kernels  182 us (99%)
    pallas_call x1, Pallas kernels, local_layer(): pl.pallas_call(lambda *refs: kernel(2 * width, *refs), out_shape=tuple((v...  180 us

profile of v6, /device:TPU:0, one launch (start us, length us, event | category | flops | bytes accessed | tf_op | source)
XLA Modules:
  0.0 183.3 jit_solution(16262072576573611416)
XLA Ops:
  1.3 180.1 %layer.1 = (bf16[4,2,128,1024]{3,2,1,0:T(8,128)(2,1)S(1)}, bf16[128,2048]{1,0:T(8,128)(2,1)S(1)}, bf16[128,2048]{1,0:T(8,128)(2,1)S(1)}) custom-call(s32[1]{0:T(128)S(6)} %copy.16.refs_0_, bf16[1024,1024]{1,0:T(8,128)(2,1)} %refs_1_.1, f32[1,1024]{1,0:T(1,128)} %bitcast.16, f32[1,1024]{1,0:T(1,128)} %bitcast.17, bf16[1024,512]{1,0:T(8,128)(2,1)} %refs_4_.1, ...), custom_call_target="tpu_custom_call" | custom-call | tf_op jit(solution)/shard_map/layer/pallas_call | solution.py:461
  181.4 1.7 results.1

commit v7 on v6

--- a/solution.py
+++ b/solution.py
@@ -45,8 +45,8 @@
 
 
 def kernel(d_model, p_hbm, x_hbm, g1_hbm, g2_hbm, wq_hbm, wk_hbm, wv_hbm, wo_hbm, wg_hbm, wu_hbm, wd_hbm, kc_hbm, vc_hbm,
-           fin, kc, vc,
-           p_ref, g1_ref, g2_ref, x, wq, wk, wv, wo, wg, wu, wd, qsend, qkeep, qrecv, sq1, sq1r, cos_b, sin_b, kt, vv, qs, kvn, kvsend, kvrecv, ob, orecv,
+           out, kc, vc,
+           p_ref, g1_ref, g2_ref, x, wq, wk, wv, wo, wg, wu, wd, qsend, qkeep, qrecv, sq1, sq1r, cos_b, sin_b, kt, vv, qs, kvn, kvsend, kvrecv, picks, ob, orecv,
            csend, ckeep, crecv, part, xrecv, mid, sq2, sq2r, hg, sums, gsend, gkeep, grecv, ab, arecv, acc,
            esend, ekeep, erecv, part2, yrecv, lsem, ssem, rsem):
     h = lax.axis_index('hid')
@@ -94,11 +94,17 @@
     def half(u):
         return pl.ds(UNITS[u][1] * UNITS[u][2] // 2, UNITS[u][2] // 2)
 
+    def own_rows(u):
+        i, part_no, n = UNITS[u]
+        return pl.ds(pl.multiple_of(i * BLK + c * HALF + part_no * (n // 2), 32), n // 2)
+
     def g_copy(u, j): return remote(gsend.at[UNITS[u][0], j, whole(u)], grecv.at[UNITS[u][0], j, whole(u)], G + CH * u + j, hid_dev)
     def a_copy(u, j): return remote(ab.at[UNITS[u][0], j, whole(u)], arecv.at[UNITS[u][0], j, whole(u)], A + CH * u + j, hid_dev)
     def e_copy(u): return remote(esend.at[UNITS[u][0], half(u)], erecv.at[UNITS[u][0], half(u)], E + u, core_dev)
     def y_copy(u): return remote(part2.at[UNITS[u][0], half(u)], yrecv.at[UNITS[u][0], half(u)], Y + u, x_dev)
-    def f_copy(u): return remote(fin.at[UNITS[u][0], 0, half(u)], fin.at[UNITS[u][0], 1, half(u)], F + u, core_dev)
+    def f_copy(u):
+        rows = own_rows(u)
+        return remote(out.at[rows], out.at[rows], F + u, core_dev)
 
     def qkv(i, send):
         xf = x[pl.ds(i * BLK, BLK), :].astype(F32)
@@ -263,7 +269,7 @@
         i = UNITS[u][0]
         y_copy(u).wait_recv()
         down = add(part2[i, half(u), :], yrecv[i, half(u), :])
-        fin[i, 0, half(u), :] = add(mid[i, 0, half(u), :], down)
+        out[own_rows(u), :] = add(mid[i, 0, half(u), :], down)
         f_copy(u).start()
 
     def f_step(u):
@@ -276,25 +282,25 @@
             return carry
         lax.fori_loop(0, CH, body, 0)
 
+    span = PAST_MAX
+
+    def make_picks():
+        at = BLK - p_ref[0] + lax.broadcasted_iota(jnp.int32, (BLK, span), 1)
+        picks[...] = jnp.where(at == lax.broadcasted_iota(jnp.int32, (BLK, span), 0), 1.0, 0.0).astype(BF16)
+
     def place(i, head, kv_t):
         lanes = pl.ds(pl.multiple_of(head * 64, 64), 64)
-
-        def tile(n, carry):
-            cols = pl.ds(pl.multiple_of(n * BLK, BLK), BLK)
-            first = (n - i) * BLK - p_ref[0]
-            at = first + lax.broadcasted_iota(jnp.int32, (BLK, BLK), 1)
-            pick = jnp.where(at == lax.broadcasted_iota(jnp.int32, (BLK, BLK), 0), 1.0, 0.0).astype(BF16)
-            new = jnp.dot(kv_t, pick, preferred_element_type=F32)
-            where = first + lax.broadcasted_iota(jnp.int32, (64, BLK), 1)
-            fresh = (where >= 0) & (where < BLK)
-            kc[lanes, cols] = jnp.where(fresh, new[:64], kc[lanes, cols].astype(F32)).astype(BF16)
-            vc[lanes, cols] = jnp.where(fresh, new[64:], vc[lanes, cols].astype(F32)).astype(BF16)
-            return carry
-        lax.fori_loop(i + 1, i + 1 + PAST_MAX // BLK, tile, 0)
+        cols = slice((i + 1) * BLK, (i + 1) * BLK + span)
+        where = BLK - p_ref[0] + lax.broadcasted_iota(jnp.int32, (1, span), 1)
+        fresh = (where >= 0) & (where < BLK)
+        new = jnp.dot(kv_t, picks[...], preferred_element_type=F32)
+        kc[lanes, cols] = jnp.where(fresh, new[:64], kc[lanes, cols].astype(F32)).astype(BF16)
+        vc[lanes, cols] = jnp.where(fresh, new[64:], vc[lanes, cols].astype(F32)).astype(BF16)
 
     def kv_step(i):
+        r = row_factor(i)
         kv_copy(i).wait_recv()
-        kv = keys_values(i, row_factor(i), qsend[i, :, 256:], kvrecv[i])
+        kv = keys_values(i, r, qsend[i, :, 256:], kvrecv[i])
         place(i, 1 - h, jnp.transpose(kv.astype(F32)).astype(BF16))
 
     for cp in ld_q:
@@ -358,6 +364,7 @@
     t_copy(3).start()
     e_step(0)
     t_copy(2).wait_recv()
+    make_picks()
     for i in range(NB):
         place(i, h, kvn[i])
     loop((u_step, 3), (v_step, 2), (w_step, 1))
@@ -400,32 +407,28 @@
     kv_step(2)
     y_step(5)
     f_step(4)
-    kv_step(3)
-    f_step(5)
-
     for i in range(NB):
-        for cp in (q_copy, r_copy, kv_copy, c_copy, x_copy, d_copy, t_copy):
+        for cp in (q_copy, r_copy, c_copy, x_copy, d_copy, t_copy):
             cp(i).wait_send()
         for n in range(2):
             o_copy(i, n).wait_send()
     for u in range(NU):
-        for cp in (e_copy, y_copy, f_copy):
-            cp(u).wait_send()
-
         def drain(j, carry, u=u):
             g_copy(u, j).wait_send()
             a_copy(u, j).wait_send()
             return carry
         lax.fori_loop(0, CH, drain, 0)
-
-
-def results_body(fin, kc, vc, out_hbm, ko_hbm, vo_hbm, sem):
-    c = lax.rem(lax.axis_index('tp'), 2)
-    copies = [pltpu.make_async_copy(kc, ko_hbm, sem.at[2 * NB]), pltpu.make_async_copy(vc, vo_hbm, sem.at[2 * NB + 1])]
+        for cp in (e_copy, y_copy, f_copy):
+            cp(u).wait_send()
+    f_step(5)
+    kv_step(3)
     for i in range(NB):
-        for k in range(2):
-            at = pl.multiple_of(i * BLK + (c if k == 0 else 1 - c) * HALF, HALF)
-            copies.append(pltpu.make_async_copy(fin.at[i, k], out_hbm.at[pl.ds(at, HALF)], sem.at[2 * i + k]))
+        kv_copy(i).wait_send()
+
+
+def results_body(out, kc, vc, out_hbm, ko_hbm, vo_hbm, sem):
+    copies = [pltpu.make_async_copy(out.at[pl.ds(i * BLK, BLK)], out_hbm.at[pl.ds(i * BLK, BLK)], sem.at[i]) for i in range(NB)]
+    copies += [pltpu.make_async_copy(kc, ko_hbm, sem.at[NB]), pltpu.make_async_copy(vc, vo_hbm, sem.at[NB + 1])]
     for cp in copies:
         cp.start()
     for cp in copies:
@@ -448,7 +451,7 @@
             v(new_len, width), v(*w_q.shape), v(*w_k.shape), v(*w_v.shape), v(*w_o.shape), v(*w_gate.shape), v(*w_up.shape), v(*w_down.shape),
             v(NB, BLK, 384), v(NB, BLK, 256), v(NB, BLK, 384), v(NB, 8, BLK, dtype=F32), v(NB, 8, BLK, dtype=F32),
             v(new_len, 128, dtype=F32), v(new_len, 128, dtype=F32), v(64, PAST_MAX + new_len), v(PAST_MAX + new_len, 64),
-            v(BLK, 256), v(NB, 128, BLK), v(NB, BLK, 128), v(NB, BLK, 128), v(NB, 2, BLK, 128), v(NB, 2, BLK, 128),
+            v(BLK, 256), v(NB, 128, BLK), v(NB, BLK, 128), v(NB, BLK, 128), v(BLK, PAST_MAX), v(NB, 2, BLK, 128), v(NB, 2, BLK, 128),
             tok, tok, tok, tok, tok, v(NB, 2, HALF, width), v(NB, 8, BLK, dtype=F32), v(NB, 8, BLK, dtype=F32), v(BLK, width), v(BLK, 128, dtype=F32),
             v(NB, CH, BLK, 2 * CW), v(2, CH, BLK, 2 * CW), v(NB, CH, BLK, 2 * CW), v(NB, CH, BLK, CW), v(NB, CH, BLK, CW),
             v(BLK, width, dtype=F32),
@@ -456,11 +459,10 @@
             pltpu.SemaphoreType.DMA((16,)),
             pltpu.SemaphoreType.DMA((N_REMOTE,)), pltpu.SemaphoreType.DMA((N_REMOTE,)),
         ]
-        kept = ((NB, 2, HALF, width), k_flat.shape, v_flat.shape)
         vmem_spec = pl.BlockSpec(memory_space=pltpu.VMEM)
         done = pl.pallas_call(
             lambda *refs: kernel(2 * width, *refs),
-            out_shape=tuple(v(*a) for a in kept),
+            out_shape=tuple(v(*a) for a in (hidden.shape, k_flat.shape, v_flat.shape)),
             in_specs=[any_spec] * 13,
             out_specs=(vmem_spec,) * 3,
             scratch_shapes=scratch,
@@ -472,7 +474,7 @@
             results_body,
             out_shape=tuple(jax.ShapeDtypeStruct(a, BF16) for a in (hidden.shape, k_flat.shape, v_flat.shape)),
             in_specs=[vmem_spec] * 3, out_specs=(any_spec,) * 3,
-            scratch_shapes=[pltpu.SemaphoreType.DMA((2 * NB + 2,))],
+            scratch_shapes=[pltpu.SemaphoreType.DMA((NB + 2,))],
             compiler_params=pltpu.CompilerParams(vmem_limit_bytes=1 << 20),
             name="results",
         )(*done)

time: 183 us -> 183 us (level)
  no operation moved by 1% of the time
where the time goes in v7:
time: 183 us
  Pallas kernels  181 us (99%)
    pallas_call x1, Pallas kernels, local_layer(): pl.pallas_call(lambda *refs: kernel(2 * width, *refs), out_shape=tuple((v...  180 us

profile of v7, /device:TPU:0, one launch (start us, length us, event | category | flops | bytes accessed | tf_op | source)
XLA Modules:
  0.0 182.8 jit_solution(6314332367865061632)
XLA Ops:
  1.3 179.6 %layer.1 = (bf16[1024,1024]{1,0:T(8,128)(2,1)S(1)}, bf16[128,2048]{1,0:T(8,128)(2,1)S(1)}, bf16[128,2048]{1,0:T(8,128)(2,1)S(1)}) custom-call(s32[1]{0:T(128)S(6)} %copy.16.refs_0_, bf16[1024,1024]{1,0:T(8,128)(2,1)} %refs_1_.1, f32[1,1024]{1,0:T(1,128)} %bitcast.16, f32[1,1024]{1,0:T(1,128)} %bitcast.17, bf16[1024,512]{1,0:T(8,128)(2,1)} %refs_4_.1, ...), custom_call_target="tpu_custom_call" | custom-call | tf_op jit(solution)/shard_map/layer/pallas_call | solution.py:463
  180.9 1.7 results.1

commit v8 on v7

--- a/solution.py
+++ b/solution.py
@@ -35,13 +35,23 @@
     return (t * cos_w + swapped * sin_w).astype(BF16)
 
 
-def row_sums(t):
-    sq = jnp.broadcast_to(jnp.sum(t * t, axis=1, keepdims=True), (t.shape[0], 128))
-    return jnp.transpose(sq)[:8]
+EPS = 1e-5
+
+
+def square_sums(t):
+    col = jnp.sum(t * t, axis=1, keepdims=True)
+    return col, jnp.transpose(jnp.broadcast_to(col, (t.shape[0], 128)))[:8]
 
 
 def as_column(row):
     return jnp.transpose(jnp.broadcast_to(row[:1], (128, row.shape[1])))[:, :1]
+
+
+def half_factors(mine, theirs, d_model):
+    r = lax.rsqrt((mine + theirs) / d_model + EPS)
+    a = mine / (d_model // 2) + EPS
+    b = theirs / (d_model // 2) + EPS
+    return as_column(r * a * lax.rsqrt(a)), as_column(r * b * lax.rsqrt(b))
 
 
 def kernel(d_model, p_hbm, x_hbm, g1_hbm, g2_hbm, wq_hbm, wk_hbm, wv_hbm, wo_hbm, wg_hbm, wu_hbm, wd_hbm, kc_hbm, vc_hbm,
@@ -108,7 +118,8 @@
 
     def qkv(i, send):
         xf = x[pl.ds(i * BLK, BLK), :].astype(F32)
-        xg = (xf * g1_ref[...]).astype(BF16)
+        sq, sq_row = square_sums(xf)
+        xg = (xf * lax.rsqrt(sq / (d_model // 2) + EPS) * g1_ref[...]).astype(BF16)
         theirs = wq[:, pl.ds(pl.multiple_of((1 - h) * 256, 256), 256)]
         qsend[i, :, :256] = jnp.dot(xg, theirs, preferred_element_type=F32).astype(BF16)
         k = jnp.dot(xg, wk[...], preferred_element_type=F32).astype(BF16)
@@ -123,7 +134,7 @@
         kvsend[i] = jnp.where(own, low, high)
         mine = wq[:, pl.ds(pl.multiple_of(h * 256, 256), 256)]
         qkeep[i] = jnp.dot(xg, mine, preferred_element_type=F32).astype(BF16)
-        sq1[i] = row_sums(xf)
+        sq1[i] = sq_row
         if send:
             r_copy(i).start()
 
@@ -136,12 +147,13 @@
         sin = jnp.sin(ang)
         sin_b[pl.ds(i * BLK, BLK), :] = jnp.where((lane & 63) < 32, -sin, sin)
 
-    def row_factor(i):
-        return as_column(lax.rsqrt((sq1[i] + sq1r[i]) / d_model + 1e-5))
-
-    def keys_values(i, r, mine, theirs):
+    def row_factors(i):
+        return half_factors(sq1[i], sq1r[i], d_model)
+
+    def keys_values(i, factors, mine, theirs):
         rows = slice(i * BLK, (i + 1) * BLK)
-        kv = ((mine.astype(F32) + theirs.astype(F32)) * r).astype(BF16)
+        mine, theirs = mine.astype(F32) * factors[0], theirs.astype(F32) * factors[1]
+        kv = (jnp.where(own, mine, theirs) + jnp.where(own, theirs, mine)).astype(BF16)
         lane = lax.broadcasted_iota(jnp.int32, kv.shape, 1)
         return jnp.where(lane < 64, rope(kv.astype(F32), cos_b[rows, :], sin_b[rows, :]), kv)
 
@@ -149,10 +161,10 @@
         rows = slice(i * BLK, (i + 1) * BLK)
         q_copy(i).wait_recv()
         r_copy(i).wait_recv()
-        r = row_factor(i)
+        factors = row_factors(i)
         cos_t, sin_t = cos_b[rows, :], sin_b[rows, :]
-        q = ((qkeep[i].astype(F32) + qrecv[i, :, :256].astype(F32)) * r).astype(BF16)
-        kv = keys_values(i, r, kvsend[i], qrecv[i, :, 256:])
+        q = (qkeep[i].astype(F32) * factors[0] + qrecv[i, :, :256].astype(F32) * factors[1]).astype(BF16)
+        kv = keys_values(i, factors, kvsend[i], qrecv[i, :, 256:])
         qs[...] = (rope(q.astype(F32), cos_t, sin_t).astype(F32) * 0.125).astype(BF16)
         kv_t = jnp.transpose(kv.astype(F32)).astype(BF16)
         kvn[i] = kv_t
@@ -217,9 +229,9 @@
             for k in range(2):
                 n = UNITS[u][2] // 2
                 m = mid[i, k, half(u), :].astype(F32)
-                sq = jnp.broadcast_to(jnp.sum(m * m, axis=1, keepdims=True), (n, 128))
-                sums[at:at + n, :] = sq
-                hg[at:at + n, :] = (m * g2_ref[...]).astype(BF16)
+                sq = jnp.sum(m * m, axis=1, keepdims=True)
+                sums[at:at + n, :] = jnp.broadcast_to(sq, (n, 128))
+                hg[at:at + n, :] = (m * lax.rsqrt(sq / (d_model // 2) + EPS) * g2_ref[...]).astype(BF16)
                 at += n
         sq2[i] = jnp.transpose(sums[...])[:8]
 
@@ -238,8 +250,10 @@
     def v_step(u, j):
         i = UNITS[u][0]
         g_copy(u, j).wait_recv()
-        r = as_column(lax.rsqrt((sq2[i] + sq2r[i]) / d_model + 1e-5))[UNITS[u][1] * UNITS[u][2]:(UNITS[u][1] + 1) * UNITS[u][2]]
-        both = ((gkeep[i % 2, j, whole(u), :].astype(F32) + grecv[i, j, whole(u), :].astype(F32)) * r).astype(BF16).astype(F32)
+        rows = slice(UNITS[u][1] * UNITS[u][2], (UNITS[u][1] + 1) * UNITS[u][2])
+        mine, theirs = (f[rows] for f in half_factors(sq2[i], sq2r[i], d_model))
+        both = gkeep[i % 2, j, whole(u), :].astype(F32) * mine + grecv[i, j, whole(u), :].astype(F32) * theirs
+        both = both.astype(BF16).astype(F32)
         g, e = both[:, :CW], both[:, CW:]
         ab[i, j, whole(u), :] = (g * jax.nn.sigmoid(g) * e).astype(BF16)
         a_copy(u, j).start()
@@ -298,9 +312,9 @@
         vc[lanes, cols] = jnp.where(fresh, new[64:], vc[lanes, cols].astype(F32)).astype(BF16)
 
     def kv_step(i):
-        r = row_factor(i)
+        factors = row_factors(i)
         kv_copy(i).wait_recv()
-        kv = keys_values(i, r, qsend[i, :, 256:], kvrecv[i])
+        kv = keys_values(i, factors, qsend[i, :, 256:], kvrecv[i])
         place(i, 1 - h, jnp.transpose(kv.astype(F32)).astype(BF16))
 
     for cp in ld_q:

time: 183 us -> 183 us (level)
  no operation moved by 1% of the time
where the time goes in v8:
time: 183 us
  Pallas kernels  182 us (99%)
    pallas_call x1, Pallas kernels, local_layer(): pl.pallas_call(lambda *refs: kernel(2 * width, *refs), out_shape=tuple((v...  180 us

profile of v8, /device:TPU:0, one launch (start us, length us, event | category | flops | bytes accessed | tf_op | source)
XLA Modules:
  0.0 183.0 jit_solution(17526309261292830879)
XLA Ops:
  1.3 179.9 %layer.1 = (bf16[1024,1024]{1,0:T(8,128)(2,1)S(1)}, bf16[128,2048]{1,0:T(8,128)(2,1)S(1)}, bf16[128,2048]{1,0:T(8,128)(2,1)S(1)}) custom-call(s32[1]{0:T(128)S(6)} %copy.16.refs_0_, bf16[1024,1024]{1,0:T(8,128)(2,1)} %refs_1_.1, f32[1,1024]{1,0:T(1,128)} %bitcast.16, f32[1,1024]{1,0:T(1,128)} %bitcast.17, bf16[1024,512]{1,0:T(8,128)(2,1)} %refs_4_.1, ...), custom_call_target="tpu_custom_call" | custom-call | tf_op jit(solution)/shard_map/layer/pallas_call | solution.py:477
  181.1 1.7 results.1

commit v9 on v8

--- a/solution.py
+++ b/solution.py
@@ -412,15 +412,15 @@
     for j in range(1, CH):
         w_step(5, j)
     e_start(5)
+    e_step(5)
     y_step(3)
-    e_step(5)
+    y_step(4)
     kv_step(0)
-    y_step(4)
+    kv_step(1)
+    y_step(5)
     f_step(3)
-    kv_step(1)
+    f_step(4)
     kv_step(2)
-    y_step(5)
-    f_step(4)
     for i in range(NB):
         for cp in (q_copy, r_copy, c_copy, x_copy, d_copy, t_copy):
             cp(i).wait_send()

time: 183 us -> 183 us (level)
  no operation moved by 1% of the time
where the time goes in v9:
time: 183 us
  Pallas kernels  181 us (99%)
    pallas_call x1, Pallas kernels, local_layer(): pl.pallas_call(lambda *refs: kernel(2 * width, *refs), out_shape=tuple((v...  180 us

profile of v9, /device:TPU:0, one launch (start us, length us, event | category | flops | bytes accessed | tf_op | source)
XLA Modules:
  0.0 182.9 jit_solution(14689445115585118524)
XLA Ops:
  1.3 179.7 %layer.1 = (bf16[1024,1024]{1,0:T(8,128)(2,1)S(1)}, bf16[128,2048]{1,0:T(8,128)(2,1)S(1)}, bf16[128,2048]{1,0:T(8,128)(2,1)S(1)}) custom-call(s32[1]{0:T(128)S(6)} %copy.16.refs_0_, bf16[1024,1024]{1,0:T(8,128)(2,1)} %refs_1_.1, f32[1,1024]{1,0:T(1,128)} %bitcast.16, f32[1,1024]{1,0:T(1,128)} %bitcast.17, bf16[1024,512]{1,0:T(8,128)(2,1)} %refs_4_.1, ...), custom_call_target="tpu_custom_call" | custom-call | tf_op jit(solution)/shard_map/layer/pallas_call | solution.py:477
  181.0 1.7 results.1

commit v10 on v9

--- a/solution.py
+++ b/solution.py
@@ -67,6 +67,10 @@
     x_dev = {'tp': lax.rem(t + 2, 4)}
     own = h == 0
 
+    barrier = pltpu.get_barrier_semaphore()
+    for dev in (hid_dev, core_dev, x_dev):
+        pl.semaphore_signal(barrier, inc=1, device_id=dev, device_id_type=MESH)
+
     loads = []
 
     def load(src, dst):
@@ -77,13 +81,13 @@
         return cp
 
     ld_x = [load(x_hbm.at[pl.ds(0, BLK)], x.at[pl.ds(0, BLK)])]
-    ld_q = [load(g1_hbm, g1_ref), load(wq_hbm, wq), load(wk_hbm, wk), load(wv_hbm, wv)]
+    q_theirs = pl.ds(pl.multiple_of((1 - h) * 256, 256), 256)
+    q_mine = pl.ds(pl.multiple_of(h * 256, 256), 256)
+    ld_q = [load(g1_hbm, g1_ref), load(wq_hbm.at[:, q_theirs], wq.at[:, q_theirs]), load(wk_hbm, wk), load(wv_hbm, wv)]
+    ld_mine = load(wq_hbm.at[:, q_mine], wq.at[:, q_mine])
     ld_x += [load(x_hbm.at[pl.ds(BLK, BLK)], x.at[pl.ds(BLK, BLK)])]
     ld_small = [load(p_hbm, p_ref), load(g2_hbm, g2_ref)]
 
-    barrier = pltpu.get_barrier_semaphore()
-    for dev in (hid_dev, core_dev, x_dev):
-        pl.semaphore_signal(barrier, inc=1, device_id=dev, device_id_type=MESH)
 
     def remote(src, dst, n, dev):
         return pltpu.make_async_remote_copy(src_ref=src, dst_ref=dst, send_sem=ssem.at[n], recv_sem=rsem.at[n],
@@ -120,7 +124,7 @@
         xf = x[pl.ds(i * BLK, BLK), :].astype(F32)
         sq, sq_row = square_sums(xf)
         xg = (xf * lax.rsqrt(sq / (d_model // 2) + EPS) * g1_ref[...]).astype(BF16)
-        theirs = wq[:, pl.ds(pl.multiple_of((1 - h) * 256, 256), 256)]
+        theirs = wq[:, q_theirs]
         qsend[i, :, :256] = jnp.dot(xg, theirs, preferred_element_type=F32).astype(BF16)
         k = jnp.dot(xg, wk[...], preferred_element_type=F32).astype(BF16)
         v = jnp.dot(xg, wv[...], preferred_element_type=F32).astype(BF16)
@@ -132,7 +136,9 @@
         if send:
             q_copy(i).start()
         kvsend[i] = jnp.where(own, low, high)
-        mine = wq[:, pl.ds(pl.multiple_of(h * 256, 256), 256)]
+        if i == 0:
+            ld_mine.wait()
+        mine = wq[:, q_mine]
         qkeep[i] = jnp.dot(xg, mine, preferred_element_type=F32).astype(BF16)
         sq1[i] = sq_row
         if send:
@@ -470,7 +476,7 @@
             v(NB, CH, BLK, 2 * CW), v(2, CH, BLK, 2 * CW), v(NB, CH, BLK, 2 * CW), v(NB, CH, BLK, CW), v(NB, CH, BLK, CW),
             v(BLK, width, dtype=F32),
             tok, tok, tok, tok, tok,
-            pltpu.SemaphoreType.DMA((16,)),
+            pltpu.SemaphoreType.DMA((17,)),
             pltpu.SemaphoreType.DMA((N_REMOTE,)), pltpu.SemaphoreType.DMA((N_REMOTE,)),
         ]
         vmem_spec = pl.BlockSpec(memory_space=pltpu.VMEM)

time: 183 us -> 183 us (level)
  no operation moved by 1% of the time
where the time goes in v10:
time: 183 us
  Pallas kernels  181 us (99%)
    pallas_call x1, Pallas kernels, local_layer(): pl.pallas_call(lambda *refs: kernel(2 * width, *refs), out_shape=tuple((v...  180 us

profile of v10, /device:TPU:0, one launch (start us, length us, event | category | flops | bytes accessed | tf_op | source)
XLA Modules:
  0.0 182.8 jit_solution(14201531526786941349)
XLA Ops:
  1.3 179.6 %layer.1 = (bf16[1024,1024]{1,0:T(8,128)(2,1)S(1)}, bf16[128,2048]{1,0:T(8,128)(2,1)S(1)}, bf16[128,2048]{1,0:T(8,128)(2,1)S(1)}) custom-call(s32[1]{0:T(128)S(6)} %copy.16.refs_0_, bf16[1024,1024]{1,0:T(8,128)(2,1)} %refs_1_.1, f32[1,1024]{1,0:T(1,128)} %bitcast.16, f32[1,1024]{1,0:T(1,128)} %bitcast.17, bf16[1024,512]{1,0:T(8,128)(2,1)} %refs_4_.1, ...), custom_call_target="tpu_custom_call" | custom-call | tf_op jit(solution)/shard_map/layer/pallas_call | solution.py:483
  180.9 1.7 results.1
